TPU v7x, 256 devices: a whole 4x4x8 slice. The times are simulated.
256 devices in a mesh: dp: 16 (over y, x), tensor: 16 (over z, core).
Axes of the slice: x: 4, y: 4, z: 8, core: 2. Of those that a mesh axis runs over, the one named last changes fastest.
Arguments:
- tokens: bfloat16 [4096, 2048], P('dp'), may hold values from -6 to 6
- gate_weight: bfloat16 [8, 2048, 2816], P(None, 'dp', 'tensor'), may hold values from -0.25 to 0.25
- up_weight: bfloat16 [8, 2048, 2816], P(None, 'dp', 'tensor'), may hold values from -0.25 to 0.25
- down_weight: bfloat16 [8, 2816, 2048], P(None, 'tensor', 'dp'), may hold values from -0.3125 to 0.3125
- router_weight: float32 [2048, 8], replicated, may hold values from -6 to 6
- carry_mean: float32 [2048], replicated, may hold values from -0.375 to 0.375
Outputs:
- mixed: bfloat16 [4096, 2048], P(('dp', 'tensor'))
All inputs are finite; a program needn't handle non-finite values.
Results may differ from a plain program's by a relative error of at most 0.028.
Values may be sent and summed in bfloat16 or wider, within the bound.
A program may use at most 64 MiB of HBM per device.

v0:
```python
import jax
import jax.numpy as jnp
from jax import lax
from jax.sharding import PartitionSpec as P

SEG = 256


soft_cap = 8.0


def copy_for_each(array, axis):
    size = lax.axis_size(axis)
    return lax.all_to_all(
        jnp.broadcast_to(array[None], (size, *array.shape)), axis, 0, 0, tiled=True
    )


def joined_along(blocks, dim):
    blocks = jnp.moveaxis(blocks, 0, dim)
    lengths = blocks.shape
    return blocks.reshape(*lengths[:dim], lengths[dim] * lengths[dim + 1], *lengths[dim + 2 :])


def gather_directly(array, axis, dim):
    blocks = copy_for_each(array, axis)
    return joined_along(blocks, dim)


def split_up(array, dim, size):
    before, after = (array.shape[:dim], array.shape[dim + 1 :])
    return jnp.moveaxis(array.reshape(*before, size, -1, *after), dim, 0)


def sent_and_summed(array, axis, dim):
    size = lax.axis_size(axis)
    blocks = lax.all_to_all(split_up(array, dim, size), axis, 0, 0, tiled=True)
    return jnp.sum(blocks.astype(jnp.float32), axis=0)


def on_device(tokens, gate_weight, up_weight, down_weight, router_weight, carry_mean):
    dp_count = lax.axis_size("dp")
    tensor_count = lax.axis_size("tensor")
    own_rows, model_width = tokens.shape
    own_segs = own_rows // SEG
    all_segs = own_segs * dp_count
    experts, slice_rows, hidden_cols = gate_weight.shape
    own_means = jnp.sum(tokens.reshape(own_segs, SEG, model_width), axis=1, dtype=jnp.float32) / SEG
    own_logits = jnp.dot(
        own_means,
        router_weight,
        precision=lax.Precision.HIGHEST,
        preferred_element_type=jnp.float32,
    )
    seg_logits = gather_directly(own_logits, "dp", 0)
    carry_logits = jnp.dot(
        carry_mean[None, :],
        router_weight,
        precision=lax.Precision.HIGHEST,
        preferred_element_type=jnp.float32,
    )
    raw_logits = jnp.concatenate([carry_logits, seg_logits[:-1]], axis=0)
    logits = soft_cap * jnp.tanh(raw_logits / soft_cap)
    scores = jnp.exp(logits)
    probs_bf = (scores / jnp.sum(scores, axis=1, keepdims=True)).astype(jnp.bfloat16)
    gate_flat = gate_weight.reshape(experts, slice_rows * hidden_cols)
    up_flat = up_weight.reshape(experts, slice_rows * hidden_cols)
    merged_gate = jnp.dot(probs_bf, gate_flat, preferred_element_type=jnp.float32).astype(
        jnp.bfloat16
    )
    merged_up = jnp.dot(probs_bf, up_flat, preferred_element_type=jnp.float32).astype(jnp.bfloat16)
    merged_both = jnp.concatenate(
        [
            merged_gate.reshape(all_segs, slice_rows, hidden_cols),
            merged_up.reshape(all_segs, slice_rows, hidden_cols),
        ],
        axis=2,
    )
    full_rows = lax.all_to_all(merged_both, "dp", split_axis=0, concat_axis=1, tiled=True)
    own_tokens = tokens.reshape(own_segs, SEG, model_width)

    def add_block(block, total):
        rows_in = lax.dynamic_slice_in_dim(own_tokens, block * slice_rows, slice_rows, 2)
        weights_in = lax.dynamic_slice_in_dim(full_rows, block * slice_rows, slice_rows, 1)
        term = jnp.einsum("str,src->stc", rows_in, weights_in, preferred_element_type=jnp.float32)
        rounded = lax.optimization_barrier(term.astype(jnp.bfloat16))
        return total + rounded.astype(jnp.float32)

    start_total = jnp.zeros((own_segs, SEG, 2 * hidden_cols), jnp.float32)
    preact = lax.fori_loop(0, dp_count, add_block, start_total).reshape(own_rows, 2 * hidden_cols)
    hidden = (jax.nn.silu(preact[:, :hidden_cols]) * preact[:, hidden_cols:]).astype(jnp.bfloat16)
    down_cols = down_weight.shape[2]
    all_hidden = gather_directly(hidden, "dp", 0)
    merged_down = jnp.dot(
        probs_bf,
        down_weight.reshape(experts, hidden_cols * down_cols),
        preferred_element_type=jnp.float32,
    )
    merged_down = merged_down.astype(jnp.bfloat16).reshape(all_segs, hidden_cols, down_cols)
    partial_value = jnp.einsum(
        "stf,sfc->stc",
        all_hidden.reshape(all_segs, SEG, hidden_cols),
        merged_down,
        preferred_element_type=jnp.float32,
    )
    block_rows = own_rows // tensor_count
    partial_value = partial_value.reshape(dp_count, tensor_count, block_rows, down_cols)
    summed = sent_and_summed(partial_value.astype(jnp.bfloat16), "tensor", 1)
    moved = lax.all_to_all(
        summed.astype(jnp.bfloat16), "dp", split_axis=0, concat_axis=3, tiled=True
    )
    return moved.reshape(block_rows, dp_count * down_cols)


def solution(mesh):
    placed = (
        P("dp", None),
        P(None, "dp", "tensor"),
        P(None, "dp", "tensor"),
        P(None, "tensor", "dp"),
        P(),
        P(),
    )
    return jax.shard_map(
        on_device, mesh=mesh, in_specs=placed, out_specs=P(("dp", "tensor"), None), check_vma=False
    )
```

profile of v0, /device:TPU:1, one launch (start us, length us, event | category | flops | bytes accessed | tf_op | source)
XLA Modules:
  0.0 147.6 jit_solution(1069213658182428304)
XLA Ops:
  0.0 1.4 convert_reduce_fusion
  1.5 0.2 convolution_bitcast_fusion
  1.7 0.7 broadcast_in_dim.7
  2.3 7.6 %all-to-all-start = ((f32[16,1,8]{2,1,0:T(1,128)}), f32[16,1,8]{2,1,0:T(1,128)S(1)}, u32[]{:S(2)}, u32[]{:S(2)}) async-start(f32[16,1,8]{2,1,0:T(1,128)} %broadcast_in_dim.7), calls=%async_computation | async-start | bytes 16384 | tf_op jit(solution)/shard_map/all_to_all | solution.py:14
  9.9 0.9 fusion.14
  10.8 1.2 copy.21
  12.1 0.7 reshape.80
  12.8 0.2 copy.22
  13.0 0.7 reshape.82
  13.7 2.6 %all-to-all-done = f32[16,1,8]{2,1,0:T(1,128)S(1)} async-done(((f32[16,1,8]{2,1,0:T(1,128)}), f32[16,1,8]{2,1,0:T(1,128)S(1)}, u32[]{:S(2)}, u32[]{:S(2)}) %all-to-all-start) | async-done | bytes 544 | tf_op jit(solution)/shard_map/all_to_all | solution.py:14
  16.4 0.1 fusion.13
  16.6 0.4 convolution_convert_fusion.3
  17.0 2.0 %reshape.81 = bf16[16,128,176]{2,1,0:T(8,128)(2,1)S(1)} reshape(bf16[16,22528]{1,0:T(8,128)(2,1)S(1)} %convolution_convert_fusion.3) | data formatting | bytes 1441792 | tf_op jit(solution)/shard_map/reshape | solution.py:74
  19.0 0.4 convolution_convert_fusion.2
  19.4 3.0 %reshape.83 = bf16[16,128,176]{2,1,0:T(8,128)(2,1)} reshape(bf16[16,22528]{1,0:T(8,128)(2,1)S(1)} %convolution_convert_fusion.2) | data formatting | bytes 1441792 | tf_op jit(solution)/shard_map/reshape | solution.py:75
  22.4 1.8 %pad_maximum_fusion = bf16[16,128,352]{2,1,0:T(8,128)(2,1)S(1)} fusion(bf16[16,128,176]{2,1,0:T(8,128)(2,1)} %reshape.83, bf16[16,128,176]{2,1,0:T(8,128)(2,1)S(1)} %reshape.81), kind=kLoop, calls=%fused_computation.12 | loop fusion | flops 2883584 | bytes 2883584 | tf_op jit(solution)/shard_map/concatenate | solution.py:72
  24.2 1.6 %copy.23 = bf16[16,128,352]{1,2,0:T(8,128)(2,1)} copy(bf16[16,128,352]{2,1,0:T(8,128)(2,1)S(1)} %pad_maximum_fusion) | data formatting | bytes 2883584 | tf_op jit(solution)/shard_map/concatenate | solution.py:72
  25.9 4.1 %all-to-all-start.1 = ((bf16[16,128,352]{1,2,0:T(8,128)(2,1)}), bf16[16,128,352]{1,2,0:T(8,128)(2,1)S(1)}, u32[]{:S(2)}, u32[]{:S(2)}) async-start(bf16[16,128,352]{1,2,0:T(8,128)(2,1)} %copy.23), calls=%async_computation.1 | async-start | bytes 2883584 | tf_op jit(solution)/shard_map/all_to_all | solution.py:79
  30.0 19.5 %all-to-all-done.1 = bf16[16,128,352]{1,2,0:T(8,128)(2,1)S(1)} async-done(((bf16[16,128,352]{1,2,0:T(8,128)(2,1)}), bf16[16,128,352]{1,2,0:T(8,128)(2,1)S(1)}, u32[]{:S(2)}, u32[]{:S(2)}) %all-to-all-start.1) | async-done | bytes 1441824 | tf_op jit(solution)/shard_map/all_to_all | solution.py:79
  49.5 0.9 copy.30
  50.3 19.8 %while.14 = (s32[]{:T(128)}, f32[1,256,352]{1,2,0:T(8,128)S(1)}, bf16[1,256,2048]{2,1,0:T(8,128)(2,1)}, bf16[1,2048,352]{2,1,0:T(8,128)(2,1)S(1)}, s32[]{:T(128)}, /*index=5*/s32[]{:T(128)}, s32[]{:T(128)}, s32[]{:T(128)}) while((s32[]{:T(128)}, f32[1,256,352]{1,2,0:T(8,128)S(1)}, bf16[1,256,2048]{2,1,0:T(8,128)(2,1)}, ...), condition=%wide.region_3.0_spmd.clone, body=%wide.region_2.0_spmd.clone.sunk | while | flops 23429124 | bytes 1246349 | solution.py:90
  50.3 1.1 fusion.31
  51.5 0.1 select_add_fusion.2
  51.6 1.1 fusion.31
  52.7 0.1 select_add_fusion.2
  52.8 1.1 fusion.31
  53.9 0.1 select_add_fusion.2
  54.1 1.1 fusion.31
  55.2 0.1 select_add_fusion.2
  55.3 1.1 fusion.31
  56.4 0.1 select_add_fusion.2
  56.5 1.1 fusion.31
  57.7 0.1 select_add_fusion.2
  57.8 1.1 fusion.31
  58.9 0.1 select_add_fusion.2
  59.0 1.1 fusion.31
  60.1 0.1 select_add_fusion.2
  60.3 1.1 fusion.31
  61.4 0.1 select_add_fusion.2
  61.5 1.1 fusion.31
  62.6 0.1 select_add_fusion.2
  62.8 1.1 fusion.31
  63.9 0.1 select_add_fusion.2
  64.0 1.1 fusion.31
  65.1 0.1 select_add_fusion.2
  65.2 1.1 fusion.31
  66.3 0.1 select_add_fusion.2
  66.5 1.1 fusion.31
  67.6 0.1 select_add_fusion.2
  67.7 1.1 fusion.31
  68.8 0.1 select_add_fusion.2
  69.0 1.1 fusion.31
  70.1 0.1 select_add_fusion.2
  70.3 1.2 broadcast_in_dim.8
  71.5 5.5 %all-to-all-start.2 = ((bf16[16,256,176]{1,2,0:T(8,128)(2,1)}), bf16[16,256,176]{1,2,0:T(8,128)(2,1)S(1)}, u32[]{:S(2)}, u32[]{:S(2)}) async-start(bf16[16,256,176]{1,2,0:T(8,128)(2,1)} %broadcast_in_dim.8), calls=%async_computation.2 | async-start | bytes 2883584 | tf_op jit(solution)/shard_map/all_to_all | solution.py:14
  76.9 0.4 fusion.6
  77.3 0.1 copy.35
  77.5 18.8 %all-to-all-done.2 = bf16[16,256,176]{1,2,0:T(8,128)(2,1)S(1)} async-done(((bf16[16,256,176]{1,2,0:T(8,128)(2,1)}), bf16[16,256,176]{1,2,0:T(8,128)(2,1)S(1)}, u32[]{:S(2)}, u32[]{:S(2)}) %all-to-all-start.2) | async-done | bytes 1441824 | tf_op jit(solution)/shard_map/all_to_all | solution.py:14
  96.2 0.8 convolution_convert_fusion.4
  97.0 0.3 copy.43
  97.3 40.4 %all_to_all.42 = bf16[16,16,1,16,128]{4,3,1,2,0:T(8,128)(2,1)S(1)} all-to-all(bf16[16,16,1,16,128]{4,3,1,2,0:T(8,128)(2,1)S(1)} %bitcast.58), channel_id=1, replica_groups=mesh['dp'=16,'tensor'=16] {'tensor'}, dimensions={0} | all-to-all | bytes 2097152 | tf_op jit(solution)/shard_map/all_to_all | solution.py:37
  137.7 0.1 reduce_sum.34
  137.8 9.1 %all_to_all.43 = bf16[16,1,16,128]{3,2,1,0:T(8,128)(2,1)S(1)} all-to-all(bf16[16,1,16,128]{3,2,1,0:T(8,128)(2,1)S(1)} %bitcast.63), channel_id=1, replica_groups=mesh['dp'=16,'tensor'=16] {'dp'}, dimensions={0} | all-to-all | bytes 131072 | tf_op jit(solution)/shard_map/all_to_all | solution.py:109
  146.9 0.6 copy.44
  (13 shorter events, 0.3 us)
Async XLA Ops:
  0.0 1.5 copy-start
  0.0 12.8 %copy-start.1 = (bf16[8,128,176]{1,2,0:T(8,128)(2,1)S(1)}, bf16[8,128,176]{1,2,0:T(8,128)(2,1)}, u32[]{:S(2)}) copy-start(bf16[8,128,176]{1,2,0:T(8,128)(2,1)} %param.10) | copy-start | bytes 1081348
  2.3 13.9 %all-to-all-start = ((f32[16,1,8]{2,1,0:T(1,128)}), f32[16,1,8]{2,1,0:T(1,128)S(1)}, u32[]{:S(2)}, u32[]{:S(2)}) async-start(f32[16,1,8]{2,1,0:T(1,128)} %broadcast_in_dim.7), calls=%async_computation | async-start | bytes 16384 | tf_op jit(solution)/shard_map/all_to_all | solution.py:14
  25.9 23.6 %all-to-all-start.1 = ((bf16[16,128,352]{1,2,0:T(8,128)(2,1)}), bf16[16,128,352]{1,2,0:T(8,128)(2,1)S(1)}, u32[]{:S(2)}, u32[]{:S(2)}) async-start(bf16[16,128,352]{1,2,0:T(8,128)(2,1)} %copy.23), calls=%async_computation.1 | async-start | bytes 2883584 | tf_op jit(solution)/shard_map/all_to_all | solution.py:79
  71.5 5.5 %copy-start.2 = (bf16[8,176,128]{2,1,0:T(8,128)(2,1)S(1)}, bf16[8,176,128]{2,1,0:T(8,128)(2,1)}, u32[]{:S(2)}) copy-start(bf16[8,176,128]{2,1,0:T(8,128)(2,1)} %param.11) | copy-start | bytes 1081348
  71.5 24.7 %all-to-all-start.2 = ((bf16[16,256,176]{1,2,0:T(8,128)(2,1)}), bf16[16,256,176]{1,2,0:T(8,128)(2,1)S(1)}, u32[]{:S(2)}, u32[]{:S(2)}) async-start(bf16[16,256,176]{1,2,0:T(8,128)(2,1)} %broadcast_in_dim.8), calls=%async_computation.2 | async-start | bytes 2883584 | tf_op jit(solution)/shard_map/all_to_all | solution.py:14
where the time goes:
time: 149 us; the launch traced here: 148 us
  blocking collectives  49.5 us (33%)
  waiting for transfers between devices  40.8 us (27%)
  matrix products  20.7 us (14%)
  starting transfers between devices  17.1 us (11%)
  local copies, waits for them, and re-layouts  13.3 us (9%)
  other arithmetic  5.29 us (4%)
    all_to_all x1, blocking collectives, sent_and_summed(): blocks = lax.all_to_all(split_up(array, dim, size), axis, 0, 0, tiled=True)  40.4 us
    all_to_all x2, waiting for transfers between devices, copy_for_each(): lax.all_to_all(jnp.broadcast_to(array[None], (size, *array.shape)), axis,...  21.3 us
    all_to_all x1, waiting for transfers between devices, on_device(): lax.all_to_all(merged_both, 'dp', split_axis=0, concat_axis=1, tiled=True)  19.5 us
    dot_general x16, matrix products, add_block(): jnp.einsum('str,src->stc', rows_in, weights_in, preferred_element_type=jn...  17.6 us
    all_to_all x2, starting transfers between devices, copy_for_each(): lax.all_to_all(jnp.broadcast_to(array[None], (size, *array.shape)), axis,...  13 us
    all_to_all x1, blocking collectives, on_device(): lax.all_to_all(summed.astype(jnp.bfloat16), 'dp', split_axis=0, concat_ax...  9.07 us
    all_to_all x1, starting transfers between devices, on_device(): lax.all_to_all(merged_both, 'dp', split_axis=0, concat_axis=1, tiled=True)  4.09 us
    unnamed x12, local copies, waits for them, and re-layouts  3.14 us
  transfers between devices with their start and end apart: 3, of which 3 were waited for; matrix products, arithmetic and copies ran while one was open for 3% of the time, Pallas kernels for 0%

commit v1 on v0

v1 whole, which is shorter than its diff:
```python
import functools

import jax
import jax.numpy as jnp
from jax import lax
from jax.experimental import pallas as pl
from jax.experimental.pallas import tpu as pltpu
from jax.sharding import PartitionSpec as P

MESH = pl.DeviceIdType.MESH
SEG = 256
CAP = 8.0
NX = 4
LANES = 128
STEP = 32

OFFSETS = (
    (2, 2), (2, 1), (2, 3), (1, 2), (3, 2), (2, 0), (0, 2),
    (1, 1), (3, 3), (1, 3), (3, 1), (1, 0), (3, 0), (0, 1), (0, 3),
)
Z_ORDER = (4, 3, 5, 2, 6, 1, 7, 0)


def kernel(
    n_dp, n_tensor,
    tok_h, gate_h, up_h, down_h, router_h, carry_h, out_ref,
    tok, weights, router, carry, row_out, row_in, prior, lhs, merged, recv,
    acc_g, acc_u, part, sib, ring_in, ring_out,
    load_sem, row_send, row_recv, gu_send, gu_recv, dn_send, dn_recv,
    sib_send, sib_recv, ring_send, ring_recv,
):
    d = lax.axis_index("dp")
    t = lax.axis_index("tensor")
    n_y = n_dp // NX
    n_z = n_tensor // 2
    x, y = lax.rem(d, NX), lax.div(d, NX)
    c, z = lax.rem(t, 2), lax.div(t, 2)
    experts = weights.shape[0]
    ff = gate_h.shape[1]

    def peer(dx, dy):
        return lax.rem(y + dy, n_y) * NX + lax.rem(x + dx, NX)

    def source(dx, dy):
        return peer(NX - dx, n_y - dy)

    def z_at(offset):
        return lax.rem(z + offset + n_z, n_z)

    sibling = z * 2 + 1 - c
    z_next = {1: z_at(1) * 2 + c, -1: z_at(-1) * 2 + c}

    loads = [
        pltpu.make_async_copy(router_h, router, load_sem.at[0]),
        pltpu.make_async_copy(carry_h, carry, load_sem.at[1]),
        pltpu.make_async_copy(tok_h, tok, load_sem.at[2]),
        pltpu.make_async_copy(gate_h, weights.at[:, 0:ff, :], load_sem.at[3]),
        pltpu.make_async_copy(up_h, weights.at[:, ff : 2 * ff, :], load_sem.at[4]),
        pltpu.make_async_copy(down_h, weights.at[:, 2 * ff : 3 * ff, :], load_sem.at[5]),
    ]
    for load in loads:
        load.start()

    barrier = pltpu.get_barrier_semaphore()
    for dx, dy in OFFSETS:
        pl.semaphore_signal(barrier, inc=1, device_id={"dp": peer(dx, dy)}, device_id_type=MESH)
    for other in (sibling, z_next[1], z_next[-1]):
        pl.semaphore_signal(barrier, inc=1, device_id={"tensor": other}, device_id_type=MESH)

    width = experts * STEP
    spread = lax.broadcasted_iota(jnp.int32, (experts, width), 1) // STEP == lax.broadcasted_iota(
        jnp.int32, (experts, width), 0
    )

    def spread_row(acc):
        total = jnp.sum(acc, axis=1, keepdims=True)
        return jnp.sum(jnp.where(spread, total, 0.0), axis=0, keepdims=True)

    loads[0].wait()
    loads[1].wait()
    blocks = tok.shape[1] // LANES
    acc = jnp.zeros((experts, LANES), jnp.float32)
    for i in range(blocks):
        acc += router[:, i * LANES : (i + 1) * LANES] * carry[i : i + 1, :]
    prior[0:1, :] = spread_row(acc)
    loads[2].wait()
    acc = jnp.zeros((experts, LANES), jnp.float32)
    for i in range(blocks):
        block = tok[:, i * LANES : (i + 1) * LANES].astype(jnp.float32)
        mean = jnp.sum(block, axis=0, keepdims=True) / SEG
        acc += router[:, i * LANES : (i + 1) * LANES] * mean
    own_row = spread_row(acc)
    row_out[...] = own_row
    row_in[d] = own_row

    pl.semaphore_wait(barrier, len(OFFSETS) + 3)

    rows = []
    for j, (dx, dy) in enumerate(OFFSETS):
        rows.append(
            pltpu.make_async_remote_copy(
                src_ref=row_out,
                dst_ref=row_in.at[d],
                send_sem=row_send.at[j],
                recv_sem=row_recv.at[j],
                device_id={"dp": peer(dx, dy)},
                device_id_type=MESH,
            )
        )
        rows[-1].start()
    for load in loads[3:]:
        load.wait()
    for copy in rows:
        copy.wait_recv()

    for s in range(n_dp - 1):
        prior[s + 1 : s + 2, :] = row_in[s]
    scores = jnp.exp(CAP * jnp.tanh(prior[...] / CAP))
    probs = scores / (jnp.sum(scores, axis=1, keepdims=True) / STEP)
    probs = probs.astype(jnp.bfloat16).astype(jnp.float32)
    diag = lax.rem(lax.broadcasted_iota(jnp.int32, (STEP, width), 1), STEP) == lax.broadcasted_iota(
        jnp.int32, (STEP, width), 0
    )
    for s in range(n_dp):
        lhs[s * STEP : (s + 1) * STEP, :] = jnp.where(diag, probs[s : s + 1, :], 0.0).astype(
            jnp.bfloat16
        )

    def merge(start):
        right = weights[:, start : start + STEP, :].reshape(width, LANES)
        both = jnp.dot(lhs[...], right, preferred_element_type=jnp.float32)
        merged[:, start : start + STEP, :] = both.astype(jnp.bfloat16).reshape(n_dp, STEP, LANES)

    def send_blocks(low, high, send_sem, recv_sem):
        copies = []
        for j, (dx, dy) in enumerate(OFFSETS):
            to = peer(dx, dy)
            copies.append(
                pltpu.make_async_remote_copy(
                    src_ref=merged.at[to, low:high, :],
                    dst_ref=recv.at[d, low:high, :],
                    send_sem=send_sem.at[j],
                    recv_sem=recv_sem.at[j],
                    device_id={"dp": to},
                    device_id_type=MESH,
                )
            )
            copies[-1].start()
        return copies

    for start in range(0, 2 * ff, STEP):
        merge(start)
    gu = send_blocks(0, 2 * ff, gu_send, gu_recv)
    starts = list(range(2 * ff, 3 * ff - STEP + 1, STEP))
    if starts[-1] + STEP < 3 * ff:
        starts.append(3 * ff - STEP)
    for start in starts:
        merge(start)
    dn = send_blocks(2 * ff, 3 * ff, dn_send, dn_recv)
    recv[d] = merged[d]

    own_first = [None] + list(range(len(OFFSETS) - 1, -1, -1))
    groups = [own_first[i : i + 4] for i in range(0, len(own_first), 4)]
    nt = (((1,), (1,)), ((), ()))
    for g, group in enumerate(groups):
        left, right_g, right_u = [], [], []
        for j in group:
            if j is None:
                src = d
            else:
                gu[j].wait_recv()
                src = source(*OFFSETS[j])
            left.append(tok[:, pl.ds(pl.multiple_of(src * LANES, LANES), LANES)])
            right_g.append(recv[src, 0:ff, :])
            right_u.append(recv[src, ff : 2 * ff, :])
        left = jnp.concatenate(left, axis=1)
        more_g = lax.dot_general(
            left, jnp.concatenate(right_g, axis=1), nt, preferred_element_type=jnp.float32
        )
        more_u = lax.dot_general(
            left, jnp.concatenate(right_u, axis=1), nt, preferred_element_type=jnp.float32
        )
        if g == 0:
            acc_g[...] = more_g
            acc_u[...] = more_u
        else:
            acc_g[...] += more_g
            acc_u[...] += more_u
    gate = acc_g[...]
    hidden = (gate / (1.0 + jnp.exp(-gate)) * acc_u[...]).astype(jnp.bfloat16)

    for copy in dn:
        copy.wait_recv()
    for i in range(0, n_dp, 2):
        right = jnp.concatenate(
            [recv[i, 2 * ff : 3 * ff, :], recv[i + 1, 2 * ff : 3 * ff, :]], axis=1
        )
        term = jnp.dot(hidden, right, preferred_element_type=jnp.float32)
        part[:, :, i * LANES : (i + 2) * LANES] = term.astype(jnp.bfloat16).reshape(
            n_tensor, SEG // n_tensor, 2 * LANES
        )

    pair = {}
    for offset in Z_ORDER:
        pair[offset] = pltpu.make_async_remote_copy(
            src_ref=part.at[z_at(offset) * 2 + 1 - c],
            dst_ref=sib.at[offset],
            send_sem=sib_send.at[offset],
            recv_sem=sib_recv.at[offset],
            device_id={"tensor": sibling},
            device_id_type=MESH,
        )
        pair[offset].start()
    half = part.shape[2] // 2
    waited = set()

    def own(offset, h):
        offset = offset % n_z
        if offset not in waited:
            pair[offset].wait_recv()
            waited.add(offset)
        cols = slice(h * half, (h + 1) * half)
        mine = part[z_at(offset) * 2 + c, :, cols].astype(jnp.float32)
        return mine + sib[offset, :, cols].astype(jnp.float32)

    far = n_z // 2
    chains = [(0, 1, far), (1, -1, far), (0, -1, far - 1), (1, 1, far - 1)]
    ring = {}
    for k in range(far):
        for i, (h, way, length) in enumerate(chains):
            if k >= length:
                continue
            value = own(way * (length - k), h)
            if k:
                ring[i, k - 1].wait_recv()
                value = value + ring_in[i, k - 1].astype(jnp.float32)
            ring_out[i, k] = value.astype(jnp.bfloat16)
            ring[i, k] = pltpu.make_async_remote_copy(
                src_ref=ring_out.at[i, k],
                dst_ref=ring_in.at[i, k],
                send_sem=ring_send.at[i, k],
                recv_sem=ring_recv.at[i, k],
                device_id={"tensor": z_next[way]},
                device_id_type=MESH,
            )
            ring[i, k].start()
    for h in range(2):
        value = own(0, h)
        for i, (of, way, length) in enumerate(chains):
            if of == h:
                ring[i, length - 1].wait_recv()
                value = value + ring_in[i, length - 1].astype(jnp.float32)
        out_ref[:, h * half : (h + 1) * half] = value.astype(jnp.bfloat16)

    for copy in rows + gu + dn + list(pair.values()) + list(ring.values()):
        copy.wait_send()


def solution(mesh):
    n_dp, n_tensor = mesh.shape["dp"], mesh.shape["tensor"]

    def on_device(tokens, gate_weight, up_weight, down_weight, router_weight, carry_mean):
        rows, width = tokens.shape
        experts, _, ff = gate_weight.shape
        n_z = n_tensor // 2
        peers = len(OFFSETS)
        block = rows // n_tensor
        any_space = pl.BlockSpec(memory_space=pl.ANY)
        bf16, f32 = jnp.bfloat16, jnp.float32
        dma = pltpu.SemaphoreType.DMA
        return pl.pallas_call(
            functools.partial(kernel, n_dp, n_tensor),
            out_shape=jax.ShapeDtypeStruct((block, width), bf16),
            in_specs=[any_space] * 6,
            out_specs=pl.BlockSpec(memory_space=pltpu.VMEM),
            scratch_shapes=[
                pltpu.VMEM((rows, width), bf16),
                pltpu.VMEM((experts, 3 * ff, LANES), bf16),
                pltpu.VMEM((experts, width), f32),
                pltpu.VMEM((width // LANES, LANES), f32),
                pltpu.VMEM((1, experts * STEP), f32),
                pltpu.VMEM((n_dp, 1, experts * STEP), f32),
                pltpu.VMEM((n_dp, experts * STEP), f32),
                pltpu.VMEM((n_dp * STEP, experts * STEP), bf16),
                pltpu.VMEM((n_dp, 3 * ff, LANES), bf16),
                pltpu.VMEM((n_dp, 3 * ff, LANES), bf16),
                pltpu.VMEM((rows, ff), f32),
                pltpu.VMEM((rows, ff), f32),
                pltpu.VMEM((n_tensor, block, width), bf16),
                pltpu.VMEM((n_z, block, width), bf16),
                pltpu.VMEM((4, n_z // 2, block, width // 2), bf16),
                pltpu.VMEM((4, n_z // 2, block, width // 2), bf16),
                dma((6,)),
                dma((peers,)), dma((peers,)),
                dma((peers,)), dma((peers,)),
                dma((peers,)), dma((peers,)),
                dma((n_z,)), dma((n_z,)),
                dma((4, n_z // 2)), dma((4, n_z // 2)),
            ],
            compiler_params=pltpu.CompilerParams(
                collective_id=0, has_side_effects=True, vmem_limit_bytes=67043328
            ),
        )(
            tokens,
            jnp.transpose(gate_weight, (0, 2, 1)),
            jnp.transpose(up_weight, (0, 2, 1)),
            down_weight,
            router_weight.T,
            carry_mean.reshape(width // LANES, LANES),
        )

    placed = (
        P("dp", None),
        P(None, "dp", "tensor"),
        P(None, "dp", "tensor"),
        P(None, "tensor", "dp"),
        P(),
        P(),
    )
    return jax.shard_map(
        on_device, mesh=mesh, in_specs=placed, out_specs=P(("dp", "tensor"), None), check_vma=False
    )
```

time: 149 us -> 56.7 us (0.38)
  Pallas kernels: 0 us -> 54.8 us
  blocking collectives: 49.5 us -> 0 us
  waiting for transfers between devices: 40.8 us -> 0 us
  matrix products: 20.7 us -> 0 us
  starting transfers between devices: 17.1 us -> 0 us
  local copies, waits for them, and re-layouts: 13.3 us -> 1.47 us
  other arithmetic: 5.29 us -> 0 us
    pallas_call x0 -> x1, Pallas kernels: none -> 54.8 us  [on_device(): pl.pallas_call(functools.partial(kernel, n_dp, n_tensor), out_shape=jax.S...]
    all_to_all x2 -> x0, blocking collectives: 49.5 us -> none  [the longest x1 40.4 us: sent_and_summed(): blocks = lax.all_to_all(split_up(array, dim, size), axis, 0, 0, tiled=True)]
    all_to_all x3 -> x0, waiting for transfers between devices: 40.8 us -> none  [the longest x2 21.3 us: copy_for_each(): lax.all_to_all(jnp.broadcast_to(array[None], (size, *array.shape)), axis,...]
    dot_general x22 -> x0, matrix products: 20.7 us -> none  [the longest x16 17.6 us: add_block(): jnp.einsum('str,src->stc', rows_in, weights_in, preferred_element_type=jn...]
    all_to_all x3 -> x0, starting transfers between devices: 17.1 us -> none  [the longest x2 13 us: copy_for_each(): lax.all_to_all(jnp.broadcast_to(array[None], (size, *array.shape)), axis,...]
    reshape x4 -> x0, local copies, waits for them, and re-layouts: 6.42 us -> none  [the longest x1 3.01 us: on_device(): merged_up.reshape(all_segs, slice_rows, hidden_cols)]
    broadcast_in_dim x2 -> x0, local copies, waits for them, and re-layouts: 1.88 us -> none  [copy_for_each(): jnp.broadcast_to(array[None], (size, *array.shape))]
    concatenate x1 -> x0, other arithmetic: 1.82 us -> none  [on_device(): jnp.concatenate([merged_gate.reshape(all_segs, slice_rows, hidden_cols),...]
  transfers between devices with their start and end apart: 3 -> 0, of which waited for: 3 -> 0; matrix products, arithmetic and copies ran while one was open for 3% -> 0% of each run, Pallas kernels for 0% -> 0%
where the time goes in v1:
time: 56.7 us; the launch traced here: 56.3 us
  Pallas kernels  54.8 us (97%)
  local copies, waits for them, and re-layouts  1.47 us (3%)
    pallas_call x1, Pallas kernels, on_device(): pl.pallas_call(functools.partial(kernel, n_dp, n_tensor), out_shape=jax.S...  54.8 us
    unnamed x1, local copies, waits for them, and re-layouts  1.47 us

profile of v1, /device:TPU:1, one launch (start us, length us, event | category | flops | bytes accessed | tf_op | source)
XLA Modules:
  0.0 56.3 jit_solution(18063800710118164492)
XLA Ops:
  0.0 54.8 %shard_map.64 = bf16[16,2048]{1,0:T(8,128)(2,1)} custom-call(bf16[256,2048]{1,0:T(8,128)(2,1)} %tok_h.1, bf16[8,176,128]{2,1,0:T(8,128)(2,1)} %bitcast.4, bf16[8,176,128]{2,1,0:T(8,128)(2,1)} %bitcast.5, bf16[8,176,128]{2,1,0:T(8,128)(2,1)} %down_h.1, f32[8,2048]{1,0:T(8,128)} %bitcast.6, f32[16,128]{1,0:T(8,128)} %bitcast.7), custom_call_target="tpu_custom_call" | custom-call | tf_op jit(solution)/shard_map/pallas_call | solution.py:271
  54.9 1.5 %copy.8 = bf16[16,2048]{1,0:T(8,128)(2,1)} copy(bf16[16,2048]{1,0:T(8,128)(2,1)} %shard_map.64) | data formatting | bytes 131072

commit v2 on v1

v2 whole, which is shorter than its diff:
```python
import functools

import jax
import jax.numpy as jnp
from jax import lax
from jax.experimental import pallas as pl
from jax.experimental.pallas import tpu as pltpu
from jax.sharding import PartitionSpec as P

MESH = pl.DeviceIdType.MESH
SEG = 256
CAP = 8.0
NX = 4
LANES = 128
STEP = 32

READY = (
    ((1, 0), (2, 0), (1, 1), (1, 3)),
    ((3, 0), (0, 1), (0, 3), (2, 1), (2, 3), (1, 2)),
    ((3, 1), (3, 3), (0, 2), (2, 2), (3, 2), (0, 0)),
)
OFFSETS = tuple(o for group in READY for o in group if o != (0, 0))
ALL = OFFSETS + ((0, 0),)
SLOTS = (((0, 0), (1, 2)), ((0, 2), (1, 0)), ((0, 1), (1, 3)), ((0, 3), (1, 1)))


def kernel(
    n_dp, n_tensor,
    tok_h, gate_h, up_h, down_h, router_h, carry_h, out_ref,
    tok, weights, router, carry, row_out, row_in, merged, recv, recv_dn,
    acc_g, acc_u, hid, part, ring_in, ring_out, fin_in, sib_out, sib_in,
    load_sem, row_send, row_recv, gu_send, gu_recv, dn_send, dn_recv, own_send,
    hid_send, hid_recv, ring_send, ring_recv, fin_send, fin_recv, sib_send, sib_recv,
):
    d = lax.axis_index("dp")
    t = lax.axis_index("tensor")
    n_y = n_dp // NX
    n_z = n_tensor // 2
    x, y = lax.rem(d, NX), lax.div(d, NX)
    c, z = lax.rem(t, 2), lax.div(t, 2)
    q = lax.rem(x + c, 2)
    experts = weights.shape[0]
    ff = gate_h.shape[1]

    def peer(dx, dy):
        return lax.rem(y + dy, n_y) * NX + lax.rem(x + dx, NX)

    def source(dx, dy):
        return lax.rem(y + n_y - dy, n_y) * NX + lax.rem(x + NX - dx, NX)

    def z_at(offset):
        return lax.rem(z + offset + n_z, n_z)

    sibling = z * 2 + 1 - c

    def copy_to(src, dst, send, recv_sem, dp=None, tensor=None):
        to = {}
        if dp is not None:
            to["dp"] = dp
        if tensor is not None:
            to["tensor"] = tensor
        return pltpu.make_async_remote_copy(
            src_ref=src, dst_ref=dst, send_sem=send, recv_sem=recv_sem,
            device_id=to, device_id_type=MESH,
        )

    loads = [
        pltpu.make_async_copy(router_h, router, load_sem.at[0]),
        pltpu.make_async_copy(carry_h, carry, load_sem.at[1]),
        pltpu.make_async_copy(tok_h, tok, load_sem.at[2]),
        pltpu.make_async_copy(gate_h, weights.at[:, 0:ff, :], load_sem.at[3]),
        pltpu.make_async_copy(up_h, weights.at[:, ff : 2 * ff, :], load_sem.at[4]),
        pltpu.make_async_copy(down_h, weights.at[:, 2 * ff : 3 * ff, :], load_sem.at[5]),
    ]
    for load in loads:
        load.start()

    barrier = pltpu.get_barrier_semaphore()
    greeted = 0
    for dx, dy in OFFSETS:
        for tensor in (t, sibling):
            pl.semaphore_signal(
                barrier, inc=1, device_id={"dp": peer(dx, dy), "tensor": tensor}, device_id_type=MESH
            )
            greeted += 1
    for tensor in (sibling, *(z_at(way) * 2 + core for way in (1, -1) for core in (0, 1))):
        pl.semaphore_signal(barrier, inc=1, device_id={"tensor": tensor}, device_id_type=MESH)
        greeted += 1

    width = experts * STEP
    spread = lax.broadcasted_iota(jnp.int32, (experts, width), 1) // STEP == lax.broadcasted_iota(
        jnp.int32, (experts, width), 0
    )
    for load in loads[:3]:
        load.wait()
    acc = jnp.zeros((experts, LANES), jnp.float32)
    for i in range(tok.shape[1] // LANES):
        block = tok[:, i * LANES : (i + 1) * LANES].astype(jnp.float32)
        mean = jnp.sum(block, axis=0, keepdims=True) / SEG
        mean = jnp.where(d == n_dp - 1, carry[i : i + 1, :], mean)
        acc += router[:, i * LANES : (i + 1) * LANES] * mean
    total = jnp.sum(acc, axis=1, keepdims=True)
    logits = CAP * jnp.tanh(total / CAP)
    scores = jnp.exp(logits)
    probs = scores / jnp.sum(scores, axis=0, keepdims=True)
    probs = probs.astype(jnp.bfloat16).astype(jnp.float32)
    own_row = jnp.sum(jnp.where(spread, probs, 0.0), axis=0, keepdims=True)
    row_out[...] = own_row
    row_in[d] = own_row

    pl.semaphore_wait(barrier, greeted)

    rows = []
    for j, (dx, dy) in enumerate(OFFSETS):
        rows.append(
            copy_to(row_out, row_in.at[d], row_send.at[j], row_recv.at[d], dp=peer(dx, dy))
        )
        rows[-1].start()
    for load in loads[3:]:
        load.wait()

    diag = lax.rem(lax.broadcasted_iota(jnp.int32, (STEP, width), 1), STEP) == lax.broadcasted_iota(
        jnp.int32, (STEP, width), 0
    )

    def merge(left, first, start):
        count = left.shape[0] // STEP
        right = weights[:, start : start + STEP, :].reshape(width, LANES)
        both = jnp.dot(left, right, preferred_element_type=jnp.float32)
        merged[first : first + count, start : start + STEP, :] = both.astype(jnp.bfloat16).reshape(
            count, STEP, LANES
        )

    gu = []
    lefts = []
    for group in READY:
        left = []
        for dx, dy in group:
            src = lax.rem(peer(dx, dy) + n_dp - 1, n_dp)

            @pl.when(src != d)
            def _():
                copy_to(row_out, row_in.at[src], row_send.at[0], row_recv.at[src], dp=src).wait_recv()

            left.append(jnp.where(diag, row_in[src], 0.0).astype(jnp.bfloat16))
        left = jnp.concatenate(left, axis=0)
        first = ALL.index(group[0])
        lefts.append((left, first))
        for start in range(0, 2 * ff, STEP):
            merge(left, first, start)
        for offset in group:
            if offset == (0, 0):
                continue
            j = OFFSETS.index(offset)
            gu.append(
                copy_to(
                    merged.at[j, 0 : 2 * ff, :], recv.at[j], gu_send.at[j], gu_recv.at[j],
                    dp=peer(*offset),
                )
            )
            gu[-1].start()

    starts = list(range(2 * ff, 3 * ff - STEP + 1, STEP))
    if starts[-1] + STEP < 3 * ff:
        starts.append(3 * ff - STEP)
    for left, first in lefts:
        for start in starts:
            merge(left, first, start)
    own_at = len(OFFSETS)
    half_rows = pl.ds(pl.multiple_of(c * ff, 16), ff)
    dn = {}
    for g, group in enumerate(SLOTS):
        for s, (a, dy) in enumerate(group):
            slot = 2 * g + s
            for dx in (2 * a, 2 * a + 1):
                if (dx, dy) == (0, 0):
                    continue
                j = OFFSETS.index((dx, dy))
                dn[dx, dy] = copy_to(
                    merged.at[j, 2 * ff : 3 * ff, :], recv_dn.at[slot, half_rows, :],
                    dn_send.at[j], dn_recv.at[slot, c],
                    dp=peer(dx, dy), tensor=z * 2 + lax.rem(x, 2),
                )
                dn[dx, dy].start()
    own_copy = copy_to(
        merged.at[own_at, 2 * ff : 3 * ff, :], recv_dn.at[0, half_rows, :],
        own_send, dn_recv.at[0, c], tensor=sibling,
    )

    @pl.when(q == 1)
    def _():
        own_copy.start()

    @pl.when(q == 0)
    def _():
        recv_dn[0, half_rows, :] = merged[own_at, 2 * ff : 3 * ff, :]

    order = [own_at] + list(range(len(OFFSETS)))
    nt = (((1,), (1,)), ((), ()))
    for g in range(0, len(order), 4):
        left, right_g, right_u = [], [], []
        for j in order[g : g + 4]:
            if j == own_at:
                src, block = d, merged.at[own_at]
            else:
                gu[j].wait_recv()
                src, block = source(*OFFSETS[j]), recv.at[j]
            left.append(tok[:, pl.ds(pl.multiple_of(src * LANES, LANES), LANES)])
            right_g.append(block[0:ff, :])
            right_u.append(block[ff : 2 * ff, :])
        left = jnp.concatenate(left, axis=1)
        more_g = lax.dot_general(
            left, jnp.concatenate(right_g, axis=1), nt, preferred_element_type=jnp.float32
        )
        more_u = lax.dot_general(
            left, jnp.concatenate(right_u, axis=1), nt, preferred_element_type=jnp.float32
        )
        if g == 0:
            acc_g[...] = more_g
            acc_u[...] = more_u
        else:
            acc_g[...] += more_g
            acc_u[...] += more_u
    gate = acc_g[...]
    hid[c] = (gate / (1.0 + jnp.exp(-gate)) * acc_u[...]).astype(jnp.bfloat16)
    swap = copy_to(hid.at[c], hid.at[c], hid_send, hid_recv, tensor=sibling)
    swap.start()
    swap.wait_recv()

    far = n_z // 2
    block = part.shape[2] // 2
    cols = part.shape[3]
    ring, fin, sib = {}, {}, {}

    def length(g, w):
        return far - (g + w) % 2

    def link(g, w, k):
        way = 1 - 2 * w
        last = length(g, w) - 1
        value = part[g, z_at(way * (last + 1 - k))]
        if k:
            ring[g, w, k - 1].wait_recv()
            value = value + ring_in[g, w, k - 1].astype(jnp.float32)
        ring_out[g, w, k] = value.astype(jnp.bfloat16)
        if k < last:
            ring[g, w, k] = copy_to(
                ring_out.at[g, w, k], ring_in.at[g, w, k],
                ring_send.at[g, w, k], ring_recv.at[g, w, k], tensor=z_at(way) * 2 + c,
            )
            ring[g, w, k].start()
        else:
            for core in range(2):
                fin[g, w, core] = copy_to(
                    ring_out.at[g, w, k, core * block : (core + 1) * block, :],
                    fin_in.at[g, w, c],
                    fin_send.at[g, w, core], fin_recv.at[g, w, c], tensor=z_at(way) * 2 + core,
                )
                fin[g, w, core].start()

    def begin(g):
        for s, (a, dy) in enumerate(SLOTS[g]):
            slot = 2 * g + s
            low = copy_to(
                merged.at[0, 2 * ff : 3 * ff, :], recv_dn.at[slot, 0:ff, :],
                dn_send.at[0], dn_recv.at[slot, 0], tensor=sibling,
            )
            high = copy_to(
                merged.at[0, 2 * ff : 3 * ff, :], recv_dn.at[slot, ff : 2 * ff, :],
                dn_send.at[0], dn_recv.at[slot, 1], tensor=sibling,
            )
            if slot:
                low.wait_recv()
                high.wait_recv()
            else:

                @pl.when((q == 1) | (c == 1))
                def _():
                    low.wait_recv()

                @pl.when((q == 1) | (c == 0))
                def _():
                    high.wait_recv()

        term = None
        for core in range(2):
            right = jnp.concatenate(
                [recv_dn[2 * g + s, core * ff : (core + 1) * ff, :] for s in range(2)], axis=1
            )
            more = jnp.dot(hid[core], right, preferred_element_type=jnp.float32)
            term = more if term is None else term + more
        part[g] = term.reshape(n_z, 2 * block, cols)

    def to_sibling(g):
        other = pl.ds(pl.multiple_of((1 - c) * block, block), block)
        sib_out[g] = part[g, z, other, :].astype(jnp.bfloat16)
        sib[g] = copy_to(
            sib_out.at[g], sib_in.at[g], sib_send.at[g], sib_recv.at[g], tensor=sibling
        )
        sib[g].start()

    n_groups = len(SLOTS)
    for tick in range(n_groups + far):
        if tick < n_groups:
            begin(tick)
        for g in range(min(tick, n_groups - 1), -1, -1):
            k = tick - g
            for w in (g % 2, 1 - g % 2):
                if k < length(g, w):
                    link(g, w, k)
            if k == 0:
                to_sibling(g)

    mine = pl.ds(pl.multiple_of(c * block, block), block)
    for g in range(n_groups):
        sib[g].wait_recv()
        from_core = [part[g, z, mine, :], sib_in[g].astype(jnp.float32)]
        for of in range(2):
            core = c if of == 0 else 1 - c
            value = from_core[of]
            for w in range(2):
                copy_to(
                    sib_out.at[g], fin_in.at[g, w, core],
                    fin_send.at[g, w, 0], fin_recv.at[g, w, core], tensor=sibling,
                ).wait_recv()
                value = value + fin_in[g, w, core].astype(jnp.float32)
            odd = lax.rem(x + core, 2)
            for s, (a, dy) in enumerate(SLOTS[g]):
                src = source(2 * a + odd, dy)
                out_ref[:, pl.ds(pl.multiple_of(src * LANES, LANES), LANES)] = value[
                    :, s * LANES : (s + 1) * LANES
                ].astype(jnp.bfloat16)

    for copy in rows + gu + list(dn.values()):
        copy.wait_send()

    @pl.when(q == 1)
    def _():
        own_copy.wait_send()

    swap.wait_send()
    for copies in (ring, fin, sib):
        for copy in copies.values():
            copy.wait_send()


def solution(mesh):
    n_dp, n_tensor = mesh.shape["dp"], mesh.shape["tensor"]

    def on_device(tokens, gate_weight, up_weight, down_weight, router_weight, carry_mean):
        rows, width = tokens.shape
        experts, _, ff = gate_weight.shape
        n_z = n_tensor // 2
        peers = len(OFFSETS)
        groups = len(SLOTS)
        block = rows // n_tensor
        cols = 2 * LANES
        bf16, f32 = jnp.bfloat16, jnp.float32
        dma = pltpu.SemaphoreType.DMA
        return pl.pallas_call(
            functools.partial(kernel, n_dp, n_tensor),
            out_shape=jax.ShapeDtypeStruct((block, width), bf16),
            in_specs=[pl.BlockSpec(memory_space=pltpu.HBM)] * 6,
            out_specs=pl.BlockSpec(memory_space=pltpu.VMEM),
            scratch_shapes=[
                pltpu.VMEM((rows, width), bf16),
                pltpu.VMEM((experts, 3 * ff, LANES), bf16),
                pltpu.VMEM((experts, width), f32),
                pltpu.VMEM((width // LANES, LANES), f32),
                pltpu.VMEM((1, experts * STEP), f32),
                pltpu.VMEM((n_dp, 1, experts * STEP), f32),
                pltpu.VMEM((n_dp, 3 * ff, LANES), bf16),
                pltpu.VMEM((peers, 2 * ff, LANES), bf16),
                pltpu.VMEM((n_dp // 2, 2 * ff, LANES), bf16),
                pltpu.VMEM((rows, ff), f32),
                pltpu.VMEM((rows, ff), f32),
                pltpu.VMEM((2, rows, ff), bf16),
                pltpu.VMEM((groups, n_z, 2 * block, cols), f32),
                pltpu.VMEM((groups, 2, n_z // 2, 2 * block, cols), bf16),
                pltpu.VMEM((groups, 2, n_z // 2, 2 * block, cols), bf16),
                pltpu.VMEM((groups, 2, 2, block, cols), bf16),
                pltpu.VMEM((groups, block, cols), bf16),
                pltpu.VMEM((groups, block, cols), bf16),
                dma((6,)),
                dma((peers,)), dma((n_dp,)),
                dma((peers,)), dma((peers,)),
                dma((peers,)), dma((n_dp // 2, 2)), dma(()),
                dma(()), dma(()),
                dma((groups, 2, n_z // 2)), dma((groups, 2, n_z // 2)),
                dma((groups, 2, 2)), dma((groups, 2, 2)),
                dma((groups,)), dma((groups,)),
            ],
            compiler_params=pltpu.CompilerParams(
                collective_id=0, has_side_effects=True, vmem_limit_bytes=67043328
            ),
        )(
            tokens,
            jnp.transpose(gate_weight, (0, 2, 1)),
            jnp.transpose(up_weight, (0, 2, 1)),
            down_weight,
            router_weight.T,
            carry_mean.reshape(width // LANES, LANES),
        )

    placed = (
        P("dp", None),
        P(None, "dp", "tensor"),
        P(None, "dp", "tensor"),
        P(None, "tensor", "dp"),
        P(),
        P(),
    )
    return jax.shard_map(
        on_device, mesh=mesh, in_specs=placed, out_specs=P(("dp", "tensor"), None), check_vma=False
    )
```

time: 56.7 us -> 61.2 us (1.079)
  the two profiles are of different devices: /device:TPU:1 before, /device:TPU:9 now
where the time goes in v2:
time: 61.2 us; the launch traced here: 61.1 us
  Pallas kernels  59.6 us (97%)
  local copies, waits for them, and re-layouts  1.47 us (2%)
    pallas_call x1, Pallas kernels, on_device(): pl.pallas_call(functools.partial(kernel, n_dp, n_tensor), out_shape=jax.S...  59.6 us
    unnamed x1, local copies, waits for them, and re-layouts  1.47 us

profile of v2, /device:TPU:9, one launch (start us, length us, event | category | flops | bytes accessed | tf_op | source)
XLA Modules:
  0.0 61.1 jit_solution(17310229378902492347)
XLA Ops:
  0.0 59.6 %shard_map.64 = bf16[16,2048]{1,0:T(8,128)(2,1)} custom-call(bf16[256,2048]{1,0:T(8,128)(2,1)} %tok_h.1, bf16[8,176,128]{2,1,0:T(8,128)(2,1)} %bitcast.4, bf16[8,176,128]{2,1,0:T(8,128)(2,1)} %bitcast.5, bf16[8,176,128]{2,1,0:T(8,128)(2,1)} %down_h.1, f32[8,2048]{1,0:T(8,128)} %bitcast.6, f32[16,128]{1,0:T(8,128)} %bitcast.7), custom_call_target="tpu_custom_call" | custom-call | tf_op jit(solution)/shard_map/pallas_call | solution.py:360
  59.6 1.5 %copy.8 = bf16[16,2048]{1,0:T(8,128)(2,1)} copy(bf16[16,2048]{1,0:T(8,128)(2,1)} %shard_map.64) | data formatting | bytes 131072

commit v3 on v2

--- a/solution.py
+++ b/solution.py
@@ -15,12 +15,12 @@
 STEP = 32
 
 READY = (
-    ((1, 0), (2, 0), (1, 1), (1, 3)),
-    ((3, 0), (0, 1), (0, 3), (2, 1), (2, 3), (1, 2)),
-    ((3, 1), (3, 3), (0, 2), (2, 2), (3, 2), (0, 0)),
+    ((2, 2), (2, 1), (2, 3), (1, 2), (3, 2), (2, 0), (0, 2), (1, 1)),
+    ((3, 3), (1, 3), (3, 1), (1, 0), (3, 0), (0, 1), (0, 3), (0, 0)),
 )
 OFFSETS = tuple(o for group in READY for o in group if o != (0, 0))
 ALL = OFFSETS + ((0, 0),)
+Z_ORDER = (4, 3, 5, 2, 6, 1, 7, 0)
 SLOTS = (((0, 0), (1, 2)), ((0, 2), (1, 0)), ((0, 1), (1, 3)), ((0, 3), (1, 1)))
 
 
@@ -28,9 +28,9 @@
     n_dp, n_tensor,
     tok_h, gate_h, up_h, down_h, router_h, carry_h, out_ref,
     tok, weights, router, carry, row_out, row_in, merged, recv, recv_dn,
-    acc_g, acc_u, hid, part, ring_in, ring_out, fin_in, sib_out, sib_in,
+    acc_g, acc_u, hid, part, red_in,
     load_sem, row_send, row_recv, gu_send, gu_recv, dn_send, dn_recv, own_send,
-    hid_send, hid_recv, ring_send, ring_recv, fin_send, fin_recv, sib_send, sib_recv,
+    hid_send, hid_recv, red_send, red_recv, round_sem,
 ):
     d = lax.axis_index("dp")
     t = lax.axis_index("tensor")
@@ -76,16 +76,11 @@
         load.start()
 
     barrier = pltpu.get_barrier_semaphore()
-    greeted = 0
     for dx, dy in OFFSETS:
-        for tensor in (t, sibling):
-            pl.semaphore_signal(
-                barrier, inc=1, device_id={"dp": peer(dx, dy), "tensor": tensor}, device_id_type=MESH
-            )
-            greeted += 1
-    for tensor in (sibling, *(z_at(way) * 2 + core for way in (1, -1) for core in (0, 1))):
+        pl.semaphore_signal(barrier, inc=1, device_id={"dp": peer(dx, dy)}, device_id_type=MESH)
+    neighbours = [z_at(1) * 2 + c, z_at(-1) * 2 + c]
+    for tensor in [sibling] + neighbours:
         pl.semaphore_signal(barrier, inc=1, device_id={"tensor": tensor}, device_id_type=MESH)
-        greeted += 1
 
     width = experts * STEP
     spread = lax.broadcasted_iota(jnp.int32, (experts, width), 1) // STEP == lax.broadcasted_iota(
@@ -108,12 +103,12 @@
     row_out[...] = own_row
     row_in[d] = own_row
 
-    pl.semaphore_wait(barrier, greeted)
+    pl.semaphore_wait(barrier, len(OFFSETS) + 3)
 
     rows = []
     for j, (dx, dy) in enumerate(OFFSETS):
         rows.append(
-            copy_to(row_out, row_in.at[d], row_send.at[j], row_recv.at[d], dp=peer(dx, dy))
+            copy_to(row_out, row_in.at[d], row_send.at[j], row_recv.at[j], dp=peer(dx, dy))
         )
         rows[-1].start()
     for load in loads[3:]:
@@ -131,17 +126,14 @@
             count, STEP, LANES
         )
 
+    for copy in rows:
+        copy.wait_recv()
     gu = []
     lefts = []
     for group in READY:
         left = []
         for dx, dy in group:
             src = lax.rem(peer(dx, dy) + n_dp - 1, n_dp)
-
-            @pl.when(src != d)
-            def _():
-                copy_to(row_out, row_in.at[src], row_send.at[0], row_recv.at[src], dp=src).wait_recv()
-
             left.append(jnp.where(diag, row_in[src], 0.0).astype(jnp.bfloat16))
         left = jnp.concatenate(left, axis=0)
         first = ALL.index(group[0])
@@ -198,6 +190,10 @@
     order = [own_at] + list(range(len(OFFSETS)))
     nt = (((1,), (1,)), ((), ()))
     for g in range(0, len(order), 4):
+        for tensor in neighbours:
+            pl.semaphore_signal(
+                round_sem.at[g // 4], inc=1, device_id={"tensor": tensor}, device_id_type=MESH
+            )
         left, right_g, right_u = [], [], []
         for j in order[g : g + 4]:
             if j == own_at:
@@ -221,42 +217,15 @@
         else:
             acc_g[...] += more_g
             acc_u[...] += more_u
+        pl.semaphore_wait(round_sem.at[g // 4], 2)
     gate = acc_g[...]
     hid[c] = (gate / (1.0 + jnp.exp(-gate)) * acc_u[...]).astype(jnp.bfloat16)
     swap = copy_to(hid.at[c], hid.at[c], hid_send, hid_recv, tensor=sibling)
     swap.start()
     swap.wait_recv()
 
-    far = n_z // 2
-    block = part.shape[2] // 2
-    cols = part.shape[3]
-    ring, fin, sib = {}, {}, {}
-
-    def length(g, w):
-        return far - (g + w) % 2
-
-    def link(g, w, k):
-        way = 1 - 2 * w
-        last = length(g, w) - 1
-        value = part[g, z_at(way * (last + 1 - k))]
-        if k:
-            ring[g, w, k - 1].wait_recv()
-            value = value + ring_in[g, w, k - 1].astype(jnp.float32)
-        ring_out[g, w, k] = value.astype(jnp.bfloat16)
-        if k < last:
-            ring[g, w, k] = copy_to(
-                ring_out.at[g, w, k], ring_in.at[g, w, k],
-                ring_send.at[g, w, k], ring_recv.at[g, w, k], tensor=z_at(way) * 2 + c,
-            )
-            ring[g, w, k].start()
-        else:
-            for core in range(2):
-                fin[g, w, core] = copy_to(
-                    ring_out.at[g, w, k, core * block : (core + 1) * block, :],
-                    fin_in.at[g, w, c],
-                    fin_send.at[g, w, core], fin_recv.at[g, w, c], tensor=z_at(way) * 2 + core,
-                )
-                fin[g, w, core].start()
+    block = part.shape[2]
+    red = {}
 
     def begin(g):
         for s, (a, dy) in enumerate(SLOTS[g]):
@@ -289,41 +258,35 @@
             )
             more = jnp.dot(hid[core], right, preferred_element_type=jnp.float32)
             term = more if term is None else term + more
-        part[g] = term.reshape(n_z, 2 * block, cols)
-
-    def to_sibling(g):
-        other = pl.ds(pl.multiple_of((1 - c) * block, block), block)
-        sib_out[g] = part[g, z, other, :].astype(jnp.bfloat16)
-        sib[g] = copy_to(
-            sib_out.at[g], sib_in.at[g], sib_send.at[g], sib_recv.at[g], tensor=sibling
-        )
-        sib[g].start()
-
-    n_groups = len(SLOTS)
-    for tick in range(n_groups + far):
-        if tick < n_groups:
-            begin(tick)
-        for g in range(min(tick, n_groups - 1), -1, -1):
-            k = tick - g
-            for w in (g % 2, 1 - g % 2):
-                if k < length(g, w):
-                    link(g, w, k)
-            if k == 0:
-                to_sibling(g)
-
-    mine = pl.ds(pl.multiple_of(c * block, block), block)
-    for g in range(n_groups):
-        sib[g].wait_recv()
-        from_core = [part[g, z, mine, :], sib_in[g].astype(jnp.float32)]
+        part[g] = term.astype(jnp.bfloat16).reshape(n_tensor, block, part.shape[3])
+        for offset in Z_ORDER:
+            for core in (0, 1):
+                if offset:
+                    to = z_at(offset) * 2 + core
+                elif core:
+                    to = sibling
+                else:
+                    continue
+                red[g, offset, core] = copy_to(
+                    part.at[g, to], red_in.at[g, offset, c],
+                    red_send.at[g, offset, core], red_recv.at[g, offset, c], tensor=to,
+                )
+                red[g, offset, core].start()
+
+    for g in range(len(SLOTS)):
+        begin(g)
+    for g in range(len(SLOTS)):
+        for offset in Z_ORDER:
+            for core in (c, 1 - c) if offset else (1 - c,):
+                copy_to(
+                    part.at[g, t], red_in.at[g, offset, core],
+                    red_send.at[g, 0, 0], red_recv.at[g, offset, core], tensor=sibling,
+                ).wait_recv()
         for of in range(2):
             core = c if of == 0 else 1 - c
-            value = from_core[of]
-            for w in range(2):
-                copy_to(
-                    sib_out.at[g], fin_in.at[g, w, core],
-                    fin_send.at[g, w, 0], fin_recv.at[g, w, core], tensor=sibling,
-                ).wait_recv()
-                value = value + fin_in[g, w, core].astype(jnp.float32)
+            value = (part[g, t] if of == 0 else red_in[g, 0, core]).astype(jnp.float32)
+            for offset in range(1, n_z):
+                value = value + red_in[g, offset, core].astype(jnp.float32)
             odd = lax.rem(x + core, 2)
             for s, (a, dy) in enumerate(SLOTS[g]):
                 src = source(2 * a + odd, dy)
@@ -339,9 +302,8 @@
         own_copy.wait_send()
 
     swap.wait_send()
-    for copies in (ring, fin, sib):
-        for copy in copies.values():
-            copy.wait_send()
+    for copy in red.values():
+        copy.wait_send()
 
 
 def solution(mesh):
@@ -375,31 +337,31 @@
                 pltpu.VMEM((rows, ff), f32),
                 pltpu.VMEM((rows, ff), f32),
                 pltpu.VMEM((2, rows, ff), bf16),
-                pltpu.VMEM((groups, n_z, 2 * block, cols), f32),
-                pltpu.VMEM((groups, 2, n_z // 2, 2 * block, cols), bf16),
-                pltpu.VMEM((groups, 2, n_z // 2, 2 * block, cols), bf16),
-                pltpu.VMEM((groups, 2, 2, block, cols), bf16),
-                pltpu.VMEM((groups, block, cols), bf16),
-                pltpu.VMEM((groups, block, cols), bf16),
+                pltpu.VMEM((groups, n_tensor, block, cols), bf16),
+                pltpu.VMEM((groups, n_z, 2, block, cols), bf16),
                 dma((6,)),
-                dma((peers,)), dma((n_dp,)),
+                dma((peers,)), dma((peers,)),
                 dma((peers,)), dma((peers,)),
                 dma((peers,)), dma((n_dp // 2, 2)), dma(()),
                 dma(()), dma(()),
-                dma((groups, 2, n_z // 2)), dma((groups, 2, n_z // 2)),
-                dma((groups, 2, 2)), dma((groups, 2, 2)),
-                dma((groups,)), dma((groups,)),
+                dma((groups, n_z, 2)), dma((groups, n_z, 2)),
+                pltpu.SemaphoreType.REGULAR((4,)),
             ],
             compiler_params=pltpu.CompilerParams(
-                collective_id=0, has_side_effects=True, vmem_limit_bytes=67043328
+                collective_id=0, has_side_effects=True, vmem_limit_bytes=32 << 20
             ),
         )(
-            tokens,
-            jnp.transpose(gate_weight, (0, 2, 1)),
-            jnp.transpose(up_weight, (0, 2, 1)),
-            down_weight,
-            router_weight.T,
-            carry_mean.reshape(width // LANES, LANES),
+            *(
+                pltpu.with_memory_space_constraint(operand, pltpu.HBM)
+                for operand in (
+                    tokens,
+                    jnp.transpose(gate_weight, (0, 2, 1)),
+                    jnp.transpose(up_weight, (0, 2, 1)),
+                    down_weight,
+                    router_weight.T,
+                    carry_mean.reshape(width // LANES, LANES),
+                )
+            )
         )
 
     placed = (

time: 61.2 us -> 53.9 us (0.88)
  the two profiles are of different devices: /device:TPU:9 before, /device:TPU:1 now
where the time goes in v3:
time: 53.9 us
  Pallas kernels  53.2 us (99%)
  local copies, waits for them, and re-layouts  0.63 us (1%)
    pallas_call x1, Pallas kernels, on_device(): pl.pallas_call(functools.partial(kernel, n_dp, n_tensor), out_shape=jax.S...  53.2 us

profile of v3, /device:TPU:1, one launch (start us, length us, event | category | flops | bytes accessed | tf_op | source)
XLA Modules:
  0.0 53.9 jit_solution(18432211383634561146)
XLA Ops:
  0.0 53.2 %shard_map.64 = bf16[16,2048]{1,0:T(8,128)(2,1)S(1)} custom-call(bf16[256,2048]{1,0:T(8,128)(2,1)} %tok_h.1, bf16[8,176,128]{2,1,0:T(8,128)(2,1)} %bitcast.4, bf16[8,176,128]{2,1,0:T(8,128)(2,1)} %bitcast.5, bf16[8,176,128]{2,1,0:T(8,128)(2,1)} %down_h.1, f32[8,2048]{1,0:T(8,128)} %bitcast.6, f32[16,128]{1,0:T(8,128)} %bitcast.7), custom_call_target="tpu_custom_call" | custom-call | tf_op jit(solution)/shard_map/pallas_call | solution.py:322
  53.2 0.6 %copy.8 = bf16[16,2048]{1,0:T(8,128)(2,1)} copy(bf16[16,2048]{1,0:T(8,128)(2,1)S(1)} %shard_map.64) | data formatting | bytes 131072

commit v4 on v3

--- a/solution.py
+++ b/solution.py
@@ -15,22 +15,22 @@
 STEP = 32
 
 READY = (
-    ((2, 2), (2, 1), (2, 3), (1, 2), (3, 2), (2, 0), (0, 2), (1, 1)),
-    ((3, 3), (1, 3), (3, 1), (1, 0), (3, 0), (0, 1), (0, 3), (0, 0)),
+    ((2, 1), (2, 3), (1, 2), (2, 0), (1, 0), (3, 0), (0, 1), (0, 3)),
+    ((2, 2), (3, 2), (0, 2), (1, 1), (3, 3), (1, 3), (3, 1), (0, 0)),
 )
 OFFSETS = tuple(o for group in READY for o in group if o != (0, 0))
 ALL = OFFSETS + ((0, 0),)
-Z_ORDER = (4, 3, 5, 2, 6, 1, 7, 0)
 SLOTS = (((0, 0), (1, 2)), ((0, 2), (1, 0)), ((0, 1), (1, 3)), ((0, 3), (1, 1)))
+SLOT_LIST = tuple(slot for group in SLOTS for slot in group)
 
 
 def kernel(
     n_dp, n_tensor,
     tok_h, gate_h, up_h, down_h, router_h, carry_h, out_ref,
     tok, weights, router, carry, row_out, row_in, merged, recv, recv_dn,
-    acc_g, acc_u, hid, part, red_in,
+    acc_g, acc_u, hid, part, via_in, via_out, red_in,
     load_sem, row_send, row_recv, gu_send, gu_recv, dn_send, dn_recv, own_send,
-    hid_send, hid_recv, red_send, red_recv, round_sem,
+    hid_send, hid_recv, via_send, via_recv, red_send, red_recv, round_sem,
 ):
     d = lax.axis_index("dp")
     t = lax.axis_index("tensor")
@@ -108,7 +108,7 @@
     rows = []
     for j, (dx, dy) in enumerate(OFFSETS):
         rows.append(
-            copy_to(row_out, row_in.at[d], row_send.at[j], row_recv.at[j], dp=peer(dx, dy))
+            copy_to(row_out, row_in.at[d], row_send.at[j], row_recv.at[d], dp=peer(dx, dy))
         )
         rows[-1].start()
     for load in loads[3:]:
@@ -126,14 +126,17 @@
             count, STEP, LANES
         )
 
-    for copy in rows:
-        copy.wait_recv()
     gu = []
     lefts = []
     for group in READY:
         left = []
         for dx, dy in group:
             src = lax.rem(peer(dx, dy) + n_dp - 1, n_dp)
+
+            @pl.when(src != d)
+            def _():
+                copy_to(row_out, row_in.at[src], row_send.at[0], row_recv.at[src], dp=src).wait_recv()
+
             left.append(jnp.where(diag, row_in[src], 0.0).astype(jnp.bfloat16))
         left = jnp.concatenate(left, axis=0)
         first = ALL.index(group[0])
@@ -163,7 +166,7 @@
     dn = {}
     for g, group in enumerate(SLOTS):
         for s, (a, dy) in enumerate(group):
-            slot = 2 * g + s
+            slot = SLOT_LIST.index((a, dy))
             for dx in (2 * a, 2 * a + 1):
                 if (dx, dy) == (0, 0):
                     continue
@@ -224,12 +227,31 @@
     swap.start()
     swap.wait_recv()
 
-    block = part.shape[2]
-    red = {}
+    block = part.shape[1]
+    via, red = {}, {}
+
+    def span(g):
+        low = sum(len(group) for group in SLOTS[:g]) * LANES
+        return slice(low, low + len(SLOTS[g]) * LANES)
+
+    def to_relay(g, n, to, hops):
+        rows_at = pl.ds(pl.multiple_of(z_at(to) * 2, 2), 2)
+        via[g, n] = copy_to(
+            part.at[rows_at, :, span(g)], via_in.at[n, :, :, span(g)],
+            via_send.at[g, n], via_recv.at[g, n], tensor=z_at(hops) * 2 + c,
+        )
+        via[g, n].start()
+
+    def to_owner(g, n, buffer, row, chip, core):
+        red[g, n, core] = copy_to(
+            buffer.at[row, :, span(g)], red_in.at[n, c, :, span(g)],
+            red_send.at[g, n, core], red_recv.at[g, n, c], tensor=z_at(chip) * 2 + core,
+        )
+        red[g, n, core].start()
 
     def begin(g):
-        for s, (a, dy) in enumerate(SLOTS[g]):
-            slot = 2 * g + s
+        for a, dy in SLOTS[g]:
+            slot = SLOT_LIST.index((a, dy))
             low = copy_to(
                 merged.at[0, 2 * ff : 3 * ff, :], recv_dn.at[slot, 0:ff, :],
                 dn_send.at[0], dn_recv.at[slot, 0], tensor=sibling,
@@ -254,39 +276,54 @@
         term = None
         for core in range(2):
             right = jnp.concatenate(
-                [recv_dn[2 * g + s, core * ff : (core + 1) * ff, :] for s in range(2)], axis=1
+                [
+                    recv_dn[SLOT_LIST.index(at), core * ff : (core + 1) * ff, :]
+                    for at in SLOTS[g]
+                ],
+                axis=1,
             )
             more = jnp.dot(hid[core], right, preferred_element_type=jnp.float32)
             term = more if term is None else term + more
-        part[g] = term.astype(jnp.bfloat16).reshape(n_tensor, block, part.shape[3])
-        for offset in Z_ORDER:
+        part[:, :, span(g)] = term.astype(jnp.bfloat16).reshape(n_tensor, block, -1)
+        to_relay(g, 2, 4, 2 - 4 * (g % 2))
+        to_relay(g, 0, 3, 1)
+        to_relay(g, 1, -3, -1)
+        for n, way in ((1, 1), (2, -1)):
             for core in (0, 1):
-                if offset:
-                    to = z_at(offset) * 2 + core
-                elif core:
-                    to = sibling
-                else:
-                    continue
-                red[g, offset, core] = copy_to(
-                    part.at[g, to], red_in.at[g, offset, c],
-                    red_send.at[g, offset, core], red_recv.at[g, offset, c], tensor=to,
-                )
-                red[g, offset, core].start()
-
-    for g in range(len(SLOTS)):
-        begin(g)
-    for g in range(len(SLOTS)):
-        for offset in Z_ORDER:
-            for core in (c, 1 - c) if offset else (1 - c,):
+                to_owner(g, n, part, z_at(way) * 2 + core, way, core)
+        red[g, 0, 0] = copy_to(
+            part.at[sibling, :, span(g)], red_in.at[0, c, :, span(g)],
+            red_send.at[g, 0, 0], red_recv.at[g, 0, c], tensor=sibling,
+        )
+        red[g, 0, 0].start()
+
+    def relay(g):
+        for n in (2, 0, 1):
+            via[g, n].wait_recv()
+        for n, way in ((0, 1), (1, -1)):
+            rows_at = pl.ds(pl.multiple_of(z_at(2 * way) * 2, 2), 2)
+            value = part[rows_at, :, span(g)].astype(jnp.float32)
+            value = value + via_in[n, :, :, span(g)].astype(jnp.float32)
+            if n == g % 2:
+                value = value + via_in[2, :, :, span(g)].astype(jnp.float32)
+            via_out[n, :, :, span(g)] = value.astype(jnp.bfloat16)
+            for core in (0, 1):
+                to_owner(g, 3 + n, via_out.at[n], core, 2 * way, core)
+
+    def finish(g):
+        for n in range(5):
+            for core in (c, 1 - c) if n else (1 - c,):
                 copy_to(
-                    part.at[g, t], red_in.at[g, offset, core],
-                    red_send.at[g, 0, 0], red_recv.at[g, offset, core], tensor=sibling,
+                    part.at[t, :, span(g)], red_in.at[n, core, :, span(g)],
+                    red_send.at[g, 0, 0], red_recv.at[g, n, core], tensor=sibling,
                 ).wait_recv()
         for of in range(2):
             core = c if of == 0 else 1 - c
-            value = (part[g, t] if of == 0 else red_in[g, 0, core]).astype(jnp.float32)
-            for offset in range(1, n_z):
-                value = value + red_in[g, offset, core].astype(jnp.float32)
+            value = (part[t, :, span(g)] if of == 0 else red_in[0, core, :, span(g)]).astype(
+                jnp.float32
+            )
+            for n in range(1, 5):
+                value = value + red_in[n, core, :, span(g)].astype(jnp.float32)
             odd = lax.rem(x + core, 2)
             for s, (a, dy) in enumerate(SLOTS[g]):
                 src = source(2 * a + odd, dy)
@@ -294,6 +331,15 @@
                     :, s * LANES : (s + 1) * LANES
                 ].astype(jnp.bfloat16)
 
+    n_groups = len(SLOTS)
+    for g in range(n_groups):
+        begin(g)
+        if g:
+            relay(g - 1)
+    relay(n_groups - 1)
+    for g in range(n_groups):
+        finish(g)
+
     for copy in rows + gu + list(dn.values()):
         copy.wait_send()
 
@@ -302,7 +348,7 @@
         own_copy.wait_send()
 
     swap.wait_send()
-    for copy in red.values():
+    for copy in list(via.values()) + list(red.values()):
         copy.wait_send()
 
 
@@ -316,7 +362,7 @@
         peers = len(OFFSETS)
         groups = len(SLOTS)
         block = rows // n_tensor
-        cols = 2 * LANES
+        cols = len(SLOT_LIST) * LANES
         bf16, f32 = jnp.bfloat16, jnp.float32
         dma = pltpu.SemaphoreType.DMA
         return pl.pallas_call(
@@ -337,14 +383,17 @@
                 pltpu.VMEM((rows, ff), f32),
                 pltpu.VMEM((rows, ff), f32),
                 pltpu.VMEM((2, rows, ff), bf16),
-                pltpu.VMEM((groups, n_tensor, block, cols), bf16),
-                pltpu.VMEM((groups, n_z, 2, block, cols), bf16),
+                pltpu.VMEM((n_tensor, block, cols), bf16),
+                pltpu.VMEM((3, 2, block, cols), bf16),
+                pltpu.VMEM((2, 2, block, cols), bf16),
+                pltpu.VMEM((5, 2, block, cols), bf16),
                 dma((6,)),
-                dma((peers,)), dma((peers,)),
+                dma((peers,)), dma((n_dp,)),
                 dma((peers,)), dma((peers,)),
                 dma((peers,)), dma((n_dp // 2, 2)), dma(()),
                 dma(()), dma(()),
-                dma((groups, n_z, 2)), dma((groups, n_z, 2)),
+                dma((groups, 3)), dma((groups, 3)),
+                dma((groups, 5, 2)), dma((groups, 5, 2)),
                 pltpu.SemaphoreType.REGULAR((4,)),
             ],
             compiler_params=pltpu.CompilerParams(

time: 53.9 us -> 56 us (1.039)
  the two profiles are of different devices: /device:TPU:1 before, /device:TPU:3 now
where the time goes in v4:
time: 56 us; the launch traced here: 55.9 us
  Pallas kernels  55.3 us (99%)
  local copies, waits for them, and re-layouts  0.63 us (1%)
    pallas_call x1, Pallas kernels, on_device(): pl.pallas_call(functools.partial(kernel, n_dp, n_tensor), out_shape=jax.S...  55.3 us

profile of v4, /device:TPU:3, one launch (start us, length us, event | category | flops | bytes accessed | tf_op | source)
XLA Modules:
  0.0 55.9 jit_solution(5648676427576628233)
XLA Ops:
  0.0 55.3 %shard_map.64 = bf16[16,2048]{1,0:T(8,128)(2,1)S(1)} custom-call(bf16[256,2048]{1,0:T(8,128)(2,1)} %tok_h.1, bf16[8,176,128]{2,1,0:T(8,128)(2,1)} %bitcast.4, bf16[8,176,128]{2,1,0:T(8,128)(2,1)} %bitcast.5, bf16[8,176,128]{2,1,0:T(8,128)(2,1)} %down_h.1, f32[8,2048]{1,0:T(8,128)} %bitcast.6, f32[16,128]{1,0:T(8,128)} %bitcast.7), custom_call_target="tpu_custom_call" | custom-call | tf_op jit(solution)/shard_map/pallas_call | solution.py:368
  55.3 0.6 %copy.8 = bf16[16,2048]{1,0:T(8,128)(2,1)} copy(bf16[16,2048]{1,0:T(8,128)(2,1)S(1)} %shard_map.64) | data formatting | bytes 131072

commit v5 on v3

--- a/solution.py
+++ b/solution.py
@@ -20,17 +20,16 @@
 )
 OFFSETS = tuple(o for group in READY for o in group if o != (0, 0))
 ALL = OFFSETS + ((0, 0),)
-Z_ORDER = (4, 3, 5, 2, 6, 1, 7, 0)
-SLOTS = (((0, 0), (1, 2)), ((0, 2), (1, 0)), ((0, 1), (1, 3)), ((0, 3), (1, 1)))
+SLOTS = (((0, 0), (1, 2), (0, 2), (1, 0)), ((0, 1), (1, 3), (0, 3), (1, 1)))
 
 
 def kernel(
     n_dp, n_tensor,
     tok_h, gate_h, up_h, down_h, router_h, carry_h, out_ref,
     tok, weights, router, carry, row_out, row_in, merged, recv, recv_dn,
-    acc_g, acc_u, hid, part, red_in,
-    load_sem, row_send, row_recv, gu_send, gu_recv, dn_send, dn_recv, own_send,
-    hid_send, hid_recv, red_send, red_recv, round_sem,
+    acc_g, acc_u, hid, part, via_in, via_out, red_in,
+    load_sem, row_send, row_recv, gu_send, gu_recv, dn_send, dn_recv, own_send, own_recv,
+    hid_send, hid_recv, via_send, via_recv, red_send, red_recv, round_sem,
 ):
     d = lax.axis_index("dp")
     t = lax.axis_index("tensor")
@@ -64,13 +63,16 @@
             device_id=to, device_id_type=MESH,
         )
 
+    def wait_all(ref, sem):
+        pltpu.make_async_copy(ref, ref, sem).wait()
+
     loads = [
         pltpu.make_async_copy(router_h, router, load_sem.at[0]),
         pltpu.make_async_copy(carry_h, carry, load_sem.at[1]),
         pltpu.make_async_copy(tok_h, tok, load_sem.at[2]),
         pltpu.make_async_copy(gate_h, weights.at[:, 0:ff, :], load_sem.at[3]),
-        pltpu.make_async_copy(up_h, weights.at[:, ff : 2 * ff, :], load_sem.at[4]),
-        pltpu.make_async_copy(down_h, weights.at[:, 2 * ff : 3 * ff, :], load_sem.at[5]),
+        pltpu.make_async_copy(up_h, weights.at[:, ff : 2 * ff, :], load_sem.at[3]),
+        pltpu.make_async_copy(down_h, weights.at[:, 2 * ff : 3 * ff, :], load_sem.at[3]),
     ]
     for load in loads:
         load.start()
@@ -105,14 +107,10 @@
 
     pl.semaphore_wait(barrier, len(OFFSETS) + 3)
 
-    rows = []
-    for j, (dx, dy) in enumerate(OFFSETS):
-        rows.append(
-            copy_to(row_out, row_in.at[d], row_send.at[j], row_recv.at[j], dp=peer(dx, dy))
-        )
-        rows[-1].start()
-    for load in loads[3:]:
-        load.wait()
+    for dx, dy in OFFSETS:
+        copy_to(row_out, row_in.at[d], row_send, row_recv, dp=peer(dx, dy)).start()
+    wait_all(weights, load_sem.at[3])
+    wait_all(row_in.at[0 : len(OFFSETS)], row_recv)
 
     diag = lax.rem(lax.broadcasted_iota(jnp.int32, (STEP, width), 1), STEP) == lax.broadcasted_iota(
         jnp.int32, (STEP, width), 0
@@ -126,9 +124,6 @@
             count, STEP, LANES
         )
 
-    for copy in rows:
-        copy.wait_recv()
-    gu = []
     lefts = []
     for group in READY:
         left = []
@@ -144,13 +139,10 @@
             if offset == (0, 0):
                 continue
             j = OFFSETS.index(offset)
-            gu.append(
-                copy_to(
-                    merged.at[j, 0 : 2 * ff, :], recv.at[j], gu_send.at[j], gu_recv.at[j],
-                    dp=peer(*offset),
-                )
-            )
-            gu[-1].start()
+            copy_to(
+                merged.at[j, 0 : 2 * ff, :], recv.at[j], gu_send, gu_recv.at[(j + 1) // 4],
+                dp=peer(*offset),
+            ).start()
 
     starts = list(range(2 * ff, 3 * ff - STEP + 1, STEP))
     if starts[-1] + STEP < 3 * ff:
@@ -160,23 +152,20 @@
             merge(left, first, start)
     own_at = len(OFFSETS)
     half_rows = pl.ds(pl.multiple_of(c * ff, 16), ff)
-    dn = {}
     for g, group in enumerate(SLOTS):
         for s, (a, dy) in enumerate(group):
-            slot = 2 * g + s
             for dx in (2 * a, 2 * a + 1):
                 if (dx, dy) == (0, 0):
                     continue
-                j = OFFSETS.index((dx, dy))
-                dn[dx, dy] = copy_to(
-                    merged.at[j, 2 * ff : 3 * ff, :], recv_dn.at[slot, half_rows, :],
-                    dn_send.at[j], dn_recv.at[slot, c],
+                copy_to(
+                    merged.at[OFFSETS.index((dx, dy)), 2 * ff : 3 * ff, :],
+                    recv_dn.at[g, s, half_rows, :],
+                    dn_send, dn_recv.at[g],
                     dp=peer(dx, dy), tensor=z * 2 + lax.rem(x, 2),
-                )
-                dn[dx, dy].start()
+                ).start()
     own_copy = copy_to(
-        merged.at[own_at, 2 * ff : 3 * ff, :], recv_dn.at[0, half_rows, :],
-        own_send, dn_recv.at[0, c], tensor=sibling,
+        merged.at[own_at, 2 * ff : 3 * ff, :], recv_dn.at[0, 0, half_rows, :],
+        own_send, own_recv, tensor=sibling,
     )
 
     @pl.when(q == 1)
@@ -185,21 +174,23 @@
 
     @pl.when(q == 0)
     def _():
-        recv_dn[0, half_rows, :] = merged[own_at, 2 * ff : 3 * ff, :]
+        recv_dn[0, 0, half_rows, :] = merged[own_at, 2 * ff : 3 * ff, :]
 
     order = [own_at] + list(range(len(OFFSETS)))
     nt = (((1,), (1,)), ((), ()))
     for g in range(0, len(order), 4):
-        for tensor in neighbours:
-            pl.semaphore_signal(
-                round_sem.at[g // 4], inc=1, device_id={"tensor": tensor}, device_id_type=MESH
-            )
+        first, last = max(g, 1) - 1, min(g + 3, len(OFFSETS))
+        if g // 4 < 2:
+            for tensor in neighbours:
+                pl.semaphore_signal(
+                    round_sem.at[g // 4], inc=1, device_id={"tensor": tensor}, device_id_type=MESH
+                )
+        wait_all(recv.at[first:last], gu_recv.at[g // 4])
         left, right_g, right_u = [], [], []
         for j in order[g : g + 4]:
             if j == own_at:
                 src, block = d, merged.at[own_at]
             else:
-                gu[j].wait_recv()
                 src, block = source(*OFFSETS[j]), recv.at[j]
             left.append(tok[:, pl.ds(pl.multiple_of(src * LANES, LANES), LANES)])
             right_g.append(block[0:ff, :])
@@ -217,7 +208,8 @@
         else:
             acc_g[...] += more_g
             acc_u[...] += more_u
-        pl.semaphore_wait(round_sem.at[g // 4], 2)
+        if g // 4 < 2:
+            pl.semaphore_wait(round_sem.at[g // 4], 2)
     gate = acc_g[...]
     hid[c] = (gate / (1.0 + jnp.exp(-gate)) * acc_u[...]).astype(jnp.bfloat16)
     swap = copy_to(hid.at[c], hid.at[c], hid_send, hid_recv, tensor=sibling)
@@ -225,68 +217,66 @@
     swap.wait_recv()
 
     block = part.shape[2]
-    red = {}
+
+    def to_owner(g, n, buffer, row, chip, core):
+        copy_to(
+            buffer.at[row], red_in.at[g, 2 * n + c], red_send, red_recv.at[g],
+            tensor=z_at(chip) * 2 + core,
+        ).start()
 
     def begin(g):
-        for s, (a, dy) in enumerate(SLOTS[g]):
-            slot = 2 * g + s
-            low = copy_to(
-                merged.at[0, 2 * ff : 3 * ff, :], recv_dn.at[slot, 0:ff, :],
-                dn_send.at[0], dn_recv.at[slot, 0], tensor=sibling,
-            )
-            high = copy_to(
-                merged.at[0, 2 * ff : 3 * ff, :], recv_dn.at[slot, ff : 2 * ff, :],
-                dn_send.at[0], dn_recv.at[slot, 1], tensor=sibling,
-            )
-            if slot:
-                low.wait_recv()
-                high.wait_recv()
-            else:
-
-                @pl.when((q == 1) | (c == 1))
-                def _():
-                    low.wait_recv()
-
-                @pl.when((q == 1) | (c == 0))
-                def _():
-                    high.wait_recv()
-
+        if g == 0:
+
+            @pl.when(q == 0)
+            def _():
+                wait_all(recv_dn.at[0, 0, half_rows, :], own_recv)
+                wait_all(recv_dn.at[0, 1:], dn_recv.at[0])
+
+            @pl.when(q == 1)
+            def _():
+                wait_all(recv_dn.at[0], dn_recv.at[0])
+
+        else:
+            wait_all(recv_dn.at[g], dn_recv.at[g])
         term = None
         for core in range(2):
             right = jnp.concatenate(
-                [recv_dn[2 * g + s, core * ff : (core + 1) * ff, :] for s in range(2)], axis=1
+                [recv_dn[g, s, core * ff : (core + 1) * ff, :] for s in range(len(SLOTS[g]))], axis=1
             )
             more = jnp.dot(hid[core], right, preferred_element_type=jnp.float32)
             term = more if term is None else term + more
-        part[g] = term.astype(jnp.bfloat16).reshape(n_tensor, block, part.shape[3])
-        for offset in Z_ORDER:
+        part[g] = term.astype(jnp.bfloat16).reshape(n_tensor, block, -1)
+        for n, owner, hops in ((2, 4, 2 - 4 * g), (0, 3, 1), (1, -3, -1)):
+            rows_at = pl.ds(pl.multiple_of(z_at(owner) * 2, 2), 2)
+            copy_to(
+                part.at[g, rows_at], via_in.at[g, n], via_send, via_recv.at[g],
+                tensor=z_at(hops) * 2 + c,
+            ).start()
+        for n, way in ((0, 1), (1, -1)):
             for core in (0, 1):
-                if offset:
-                    to = z_at(offset) * 2 + core
-                elif core:
-                    to = sibling
-                else:
-                    continue
-                red[g, offset, core] = copy_to(
-                    part.at[g, to], red_in.at[g, offset, c],
-                    red_send.at[g, offset, core], red_recv.at[g, offset, c], tensor=to,
-                )
-                red[g, offset, core].start()
-
-    for g in range(len(SLOTS)):
-        begin(g)
-    for g in range(len(SLOTS)):
-        for offset in Z_ORDER:
-            for core in (c, 1 - c) if offset else (1 - c,):
-                copy_to(
-                    part.at[g, t], red_in.at[g, offset, core],
-                    red_send.at[g, 0, 0], red_recv.at[g, offset, core], tensor=sibling,
-                ).wait_recv()
+                to_owner(g, n, part.at[g], z_at(way) * 2 + core, way, core)
+        copy_to(
+            part.at[g, sibling], red_in.at[g, 8], red_send, red_recv.at[g], tensor=sibling
+        ).start()
+
+    def relay(g):
+        wait_all(via_in.at[g], via_recv.at[g])
+        for n, way in ((0, 1), (1, -1)):
+            rows_at = pl.ds(pl.multiple_of(z_at(2 * way) * 2, 2), 2)
+            value = part[g, rows_at].astype(jnp.float32) + via_in[g, n].astype(jnp.float32)
+            if n == g:
+                value = value + via_in[g, 2].astype(jnp.float32)
+            via_out[g, n] = value.astype(jnp.bfloat16)
+            for core in (0, 1):
+                to_owner(g, 2 + n, via_out.at[g, n], core, 2 * way, core)
+
+    def finish(g):
+        wait_all(red_in.at[g], red_recv.at[g])
         for of in range(2):
             core = c if of == 0 else 1 - c
-            value = (part[g, t] if of == 0 else red_in[g, 0, core]).astype(jnp.float32)
-            for offset in range(1, n_z):
-                value = value + red_in[g, offset, core].astype(jnp.float32)
+            value = (part[g, t] if of == 0 else red_in[g, 8]).astype(jnp.float32)
+            for n in range(4):
+                value = value + red_in[g, 2 * n + core].astype(jnp.float32)
             odd = lax.rem(x + core, 2)
             for s, (a, dy) in enumerate(SLOTS[g]):
                 src = source(2 * a + odd, dy)
@@ -294,16 +284,26 @@
                     :, s * LANES : (s + 1) * LANES
                 ].astype(jnp.bfloat16)
 
-    for copy in rows + gu + list(dn.values()):
-        copy.wait_send()
+    n_groups = len(SLOTS)
+    for g in range(n_groups):
+        begin(g)
+    for g in range(n_groups):
+        relay(g)
+    for g in range(n_groups):
+        finish(g)
+
+    peers = len(OFFSETS)
+    wait_all(row_in.at[0:peers], row_send)
+    wait_all(merged.at[0:peers, 0 : 2 * ff, :], gu_send)
+    wait_all(merged.at[0:peers, 2 * ff : 3 * ff, :], dn_send)
+    wait_all(via_in, via_send)
+    wait_all(red_in, red_send)
 
     @pl.when(q == 1)
     def _():
         own_copy.wait_send()
 
     swap.wait_send()
-    for copy in red.values():
-        copy.wait_send()
 
 
 def solution(mesh):
@@ -312,11 +312,11 @@
     def on_device(tokens, gate_weight, up_weight, down_weight, router_weight, carry_mean):
         rows, width = tokens.shape
         experts, _, ff = gate_weight.shape
-        n_z = n_tensor // 2
         peers = len(OFFSETS)
         groups = len(SLOTS)
         block = rows // n_tensor
-        cols = 2 * LANES
+        slots = len(SLOTS[0])
+        cols = slots * LANES
         bf16, f32 = jnp.bfloat16, jnp.float32
         dma = pltpu.SemaphoreType.DMA
         return pl.pallas_call(
@@ -333,19 +333,22 @@
                 pltpu.VMEM((n_dp, 1, experts * STEP), f32),
                 pltpu.VMEM((n_dp, 3 * ff, LANES), bf16),
                 pltpu.VMEM((peers, 2 * ff, LANES), bf16),
-                pltpu.VMEM((n_dp // 2, 2 * ff, LANES), bf16),
+                pltpu.VMEM((groups, slots, 2 * ff, LANES), bf16),
                 pltpu.VMEM((rows, ff), f32),
                 pltpu.VMEM((rows, ff), f32),
                 pltpu.VMEM((2, rows, ff), bf16),
                 pltpu.VMEM((groups, n_tensor, block, cols), bf16),
-                pltpu.VMEM((groups, n_z, 2, block, cols), bf16),
-                dma((6,)),
-                dma((peers,)), dma((peers,)),
-                dma((peers,)), dma((peers,)),
-                dma((peers,)), dma((n_dp // 2, 2)), dma(()),
+                pltpu.VMEM((groups, 3, 2, block, cols), bf16),
+                pltpu.VMEM((groups, 2, 2, block, cols), bf16),
+                pltpu.VMEM((groups, 9, block, cols), bf16),
+                dma((4,)),
                 dma(()), dma(()),
-                dma((groups, n_z, 2)), dma((groups, n_z, 2)),
-                pltpu.SemaphoreType.REGULAR((4,)),
+                dma(()), dma((4,)),
+                dma(()), dma((groups,)), dma(()), dma(()),
+                dma(()), dma(()),
+                dma(()), dma((groups,)),
+                dma(()), dma((groups,)),
+                pltpu.SemaphoreType.REGULAR((2,)),
             ],
             compiler_params=pltpu.CompilerParams(
                 collective_id=0, has_side_effects=True, vmem_limit_bytes=32 << 20

time: 53.9 us -> 50.8 us (0.942)
  Pallas kernels: 53.2 us -> 50 us
    pallas_call x1, Pallas kernels: 53.2 us -> 50 us  [on_device(): pl.pallas_call(functools.partial(kernel, n_dp, n_tensor), out_shape=jax.S...]
where the time goes in v5:
time: 50.8 us; the launch traced here: 50.7 us
  Pallas kernels  50 us (98%)
  local copies, waits for them, and re-layouts  0.63 us (1%)
    pallas_call x1, Pallas kernels, on_device(): pl.pallas_call(functools.partial(kernel, n_dp, n_tensor), out_shape=jax.S...  50 us

profile of v5, /device:TPU:1, one launch (start us, length us, event | category | flops | bytes accessed | tf_op | source)
XLA Modules:
  0.0 50.7 jit_solution(17863461181673838990)
XLA Ops:
  0.0 50.0 %shard_map.64 = bf16[16,2048]{1,0:T(8,128)(2,1)S(1)} custom-call(bf16[256,2048]{1,0:T(8,128)(2,1)} %tok_h.1, bf16[8,176,128]{2,1,0:T(8,128)(2,1)} %bitcast.4, bf16[8,176,128]{2,1,0:T(8,128)(2,1)} %bitcast.5, bf16[8,176,128]{2,1,0:T(8,128)(2,1)} %down_h.1, f32[8,2048]{1,0:T(8,128)} %bitcast.6, f32[16,128]{1,0:T(8,128)} %bitcast.7), custom_call_target="tpu_custom_call" | custom-call | tf_op jit(solution)/shard_map/pallas_call | solution.py:322
  50.1 0.6 %copy.8 = bf16[16,2048]{1,0:T(8,128)(2,1)} copy(bf16[16,2048]{1,0:T(8,128)(2,1)S(1)} %shard_map.64) | data formatting | bytes 131072

commit v6 on v5

--- a/solution.py
+++ b/solution.py
@@ -20,7 +20,9 @@
 )
 OFFSETS = tuple(o for group in READY for o in group if o != (0, 0))
 ALL = OFFSETS + ((0, 0),)
-SLOTS = (((0, 0), (1, 2), (0, 2), (1, 0)), ((0, 1), (1, 3), (0, 3), (1, 1)))
+SLOTS = (((0, 0), (1, 2), (0, 2), (1, 0)), ((0, 1), (1, 3), (0, 3)), ((1, 1),))
+DIRECT = (2,)
+FIRST = tuple(sum(len(group) for group in SLOTS[:g]) for g in range(len(SLOTS) + 1))
 
 
 def kernel(
@@ -159,12 +161,12 @@
                     continue
                 copy_to(
                     merged.at[OFFSETS.index((dx, dy)), 2 * ff : 3 * ff, :],
-                    recv_dn.at[g, s, half_rows, :],
+                    recv_dn.at[FIRST[g] + s, half_rows, :],
                     dn_send, dn_recv.at[g],
                     dp=peer(dx, dy), tensor=z * 2 + lax.rem(x, 2),
                 ).start()
     own_copy = copy_to(
-        merged.at[own_at, 2 * ff : 3 * ff, :], recv_dn.at[0, 0, half_rows, :],
+        merged.at[own_at, 2 * ff : 3 * ff, :], recv_dn.at[0, half_rows, :],
         own_send, own_recv, tensor=sibling,
     )
 
@@ -174,17 +176,16 @@
 
     @pl.when(q == 0)
     def _():
-        recv_dn[0, 0, half_rows, :] = merged[own_at, 2 * ff : 3 * ff, :]
+        recv_dn[0, half_rows, :] = merged[own_at, 2 * ff : 3 * ff, :]
 
     order = [own_at] + list(range(len(OFFSETS)))
     nt = (((1,), (1,)), ((), ()))
     for g in range(0, len(order), 4):
         first, last = max(g, 1) - 1, min(g + 3, len(OFFSETS))
-        if g // 4 < 2:
-            for tensor in neighbours:
-                pl.semaphore_signal(
-                    round_sem.at[g // 4], inc=1, device_id={"tensor": tensor}, device_id_type=MESH
-                )
+        for tensor in neighbours:
+            pl.semaphore_signal(
+                round_sem.at[g // 4], inc=1, device_id={"tensor": tensor}, device_id_type=MESH
+            )
         wait_all(recv.at[first:last], gu_recv.at[g // 4])
         left, right_g, right_u = [], [], []
         for j in order[g : g + 4]:
@@ -208,19 +209,22 @@
         else:
             acc_g[...] += more_g
             acc_u[...] += more_u
-        if g // 4 < 2:
-            pl.semaphore_wait(round_sem.at[g // 4], 2)
+        pl.semaphore_wait(round_sem.at[g // 4], 2)
     gate = acc_g[...]
     hid[c] = (gate / (1.0 + jnp.exp(-gate)) * acc_u[...]).astype(jnp.bfloat16)
     swap = copy_to(hid.at[c], hid.at[c], hid_send, hid_recv, tensor=sibling)
     swap.start()
     swap.wait_recv()
 
-    block = part.shape[2]
+    block = part.shape[1]
+    n_groups = len(SLOTS)
+    spans = [slice(FIRST[g] * LANES, FIRST[g + 1] * LANES) for g in range(n_groups)]
+    places = [2 * n_z - 2 if g in DIRECT else 8 for g in range(n_groups)]
 
     def to_owner(g, n, buffer, row, chip, core):
         copy_to(
-            buffer.at[row], red_in.at[g, 2 * n + c], red_send, red_recv.at[g],
+            buffer.at[row, :, spans[g]], red_in.at[1 + 2 * n + c, :, spans[g]],
+            red_send.at[g], red_recv.at[g],
             tensor=z_at(chip) * 2 + core,
         ).start()
 
@@ -229,54 +233,62 @@
 
             @pl.when(q == 0)
             def _():
-                wait_all(recv_dn.at[0, 0, half_rows, :], own_recv)
-                wait_all(recv_dn.at[0, 1:], dn_recv.at[0])
+                wait_all(recv_dn.at[0, half_rows, :], own_recv)
+                wait_all(recv_dn.at[1 : FIRST[1]], dn_recv.at[0])
 
             @pl.when(q == 1)
             def _():
-                wait_all(recv_dn.at[0], dn_recv.at[0])
+                wait_all(recv_dn.at[0 : FIRST[1]], dn_recv.at[0])
 
         else:
-            wait_all(recv_dn.at[g], dn_recv.at[g])
+            wait_all(recv_dn.at[FIRST[g] : FIRST[g + 1]], dn_recv.at[g])
         term = None
         for core in range(2):
             right = jnp.concatenate(
-                [recv_dn[g, s, core * ff : (core + 1) * ff, :] for s in range(len(SLOTS[g]))], axis=1
+                [recv_dn[s, core * ff : (core + 1) * ff, :] for s in range(FIRST[g], FIRST[g + 1])],
+                axis=1,
             )
             more = jnp.dot(hid[core], right, preferred_element_type=jnp.float32)
             term = more if term is None else term + more
-        part[g] = term.astype(jnp.bfloat16).reshape(n_tensor, block, -1)
-        for n, owner, hops in ((2, 4, 2 - 4 * g), (0, 3, 1), (1, -3, -1)):
-            rows_at = pl.ds(pl.multiple_of(z_at(owner) * 2, 2), 2)
-            copy_to(
-                part.at[g, rows_at], via_in.at[g, n], via_send, via_recv.at[g],
-                tensor=z_at(hops) * 2 + c,
-            ).start()
-        for n, way in ((0, 1), (1, -1)):
+        part[:, :, spans[g]] = term.astype(jnp.bfloat16).reshape(n_tensor, block, -1)
+        if g in DIRECT:
+            ways = (4, 3, -3, 2, -2, 1, -1)
+        else:
+            for n, owner, hops in ((2, 4, 2 - 4 * (g % 2)), (0, 3, 1), (1, -3, -1)):
+                rows_at = pl.ds(pl.multiple_of(z_at(owner) * 2, 2), 2)
+                copy_to(
+                    part.at[rows_at, :, spans[g]], via_in.at[n, :, :, spans[g]],
+                    via_send.at[g], via_recv.at[g], tensor=z_at(hops) * 2 + c,
+                ).start()
+            ways = (1, -1)
+        for n, way in enumerate(ways):
             for core in (0, 1):
-                to_owner(g, n, part.at[g], z_at(way) * 2 + core, way, core)
+                to_owner(g, n, part, z_at(way) * 2 + core, way, core)
         copy_to(
-            part.at[g, sibling], red_in.at[g, 8], red_send, red_recv.at[g], tensor=sibling
+            part.at[sibling, :, spans[g]], red_in.at[0, :, spans[g]],
+            red_send.at[g], red_recv.at[g], tensor=sibling,
         ).start()
 
     def relay(g):
-        wait_all(via_in.at[g], via_recv.at[g])
+        wait_all(via_in.at[:, :, :, spans[g]], via_recv.at[g])
         for n, way in ((0, 1), (1, -1)):
             rows_at = pl.ds(pl.multiple_of(z_at(2 * way) * 2, 2), 2)
-            value = part[g, rows_at].astype(jnp.float32) + via_in[g, n].astype(jnp.float32)
-            if n == g:
-                value = value + via_in[g, 2].astype(jnp.float32)
-            via_out[g, n] = value.astype(jnp.bfloat16)
+            value = part[rows_at, :, spans[g]].astype(jnp.float32)
+            value = value + via_in[n, :, :, spans[g]].astype(jnp.float32)
+            if n == g % 2:
+                value = value + via_in[2, :, :, spans[g]].astype(jnp.float32)
+            via_out[n, :, :, spans[g]] = value.astype(jnp.bfloat16)
             for core in (0, 1):
-                to_owner(g, 2 + n, via_out.at[g, n], core, 2 * way, core)
+                to_owner(g, 2 + n, via_out.at[n], core, 2 * way, core)
 
     def finish(g):
-        wait_all(red_in.at[g], red_recv.at[g])
+        wait_all(red_in.at[0 : 1 + places[g], :, spans[g]], red_recv.at[g])
         for of in range(2):
             core = c if of == 0 else 1 - c
-            value = (part[g, t] if of == 0 else red_in[g, 8]).astype(jnp.float32)
-            for n in range(4):
-                value = value + red_in[g, 2 * n + core].astype(jnp.float32)
+            value = part[t, :, spans[g]] if of == 0 else red_in[0, :, spans[g]]
+            value = value.astype(jnp.float32)
+            for n in range(places[g] // 2):
+                value = value + red_in[1 + 2 * n + core, :, spans[g]].astype(jnp.float32)
             odd = lax.rem(x + core, 2)
             for s, (a, dy) in enumerate(SLOTS[g]):
                 src = source(2 * a + odd, dy)
@@ -284,11 +296,11 @@
                     :, s * LANES : (s + 1) * LANES
                 ].astype(jnp.bfloat16)
 
-    n_groups = len(SLOTS)
     for g in range(n_groups):
         begin(g)
     for g in range(n_groups):
-        relay(g)
+        if g not in DIRECT:
+            relay(g)
     for g in range(n_groups):
         finish(g)
 
@@ -296,8 +308,10 @@
     wait_all(row_in.at[0:peers], row_send)
     wait_all(merged.at[0:peers, 0 : 2 * ff, :], gu_send)
     wait_all(merged.at[0:peers, 2 * ff : 3 * ff, :], dn_send)
-    wait_all(via_in, via_send)
-    wait_all(red_in, red_send)
+    for g in range(n_groups):
+        if g not in DIRECT:
+            wait_all(via_in.at[:, :, :, spans[g]], via_send.at[g])
+        wait_all(red_in.at[0 : 1 + places[g], :, spans[g]], red_send.at[g])
 
     @pl.when(q == 1)
     def _():
@@ -315,7 +329,7 @@
         peers = len(OFFSETS)
         groups = len(SLOTS)
         block = rows // n_tensor
-        slots = len(SLOTS[0])
+        slots = FIRST[-1]
         cols = slots * LANES
         bf16, f32 = jnp.bfloat16, jnp.float32
         dma = pltpu.SemaphoreType.DMA
@@ -333,22 +347,22 @@
                 pltpu.VMEM((n_dp, 1, experts * STEP), f32),
                 pltpu.VMEM((n_dp, 3 * ff, LANES), bf16),
                 pltpu.VMEM((peers, 2 * ff, LANES), bf16),
-                pltpu.VMEM((groups, slots, 2 * ff, LANES), bf16),
+                pltpu.VMEM((slots, 2 * ff, LANES), bf16),
                 pltpu.VMEM((rows, ff), f32),
                 pltpu.VMEM((rows, ff), f32),
                 pltpu.VMEM((2, rows, ff), bf16),
-                pltpu.VMEM((groups, n_tensor, block, cols), bf16),
-                pltpu.VMEM((groups, 3, 2, block, cols), bf16),
-                pltpu.VMEM((groups, 2, 2, block, cols), bf16),
-                pltpu.VMEM((groups, 9, block, cols), bf16),
+                pltpu.VMEM((n_tensor, block, cols), bf16),
+                pltpu.VMEM((3, 2, block, cols), bf16),
+                pltpu.VMEM((2, 2, block, cols), bf16),
+                pltpu.VMEM((n_tensor - 1, block, cols), bf16),
                 dma((4,)),
                 dma(()), dma(()),
                 dma(()), dma((4,)),
                 dma(()), dma((groups,)), dma(()), dma(()),
                 dma(()), dma(()),
-                dma(()), dma((groups,)),
-                dma(()), dma((groups,)),
-                pltpu.SemaphoreType.REGULAR((2,)),
+                dma((groups,)), dma((groups,)),
+                dma((groups,)), dma((groups,)),
+                pltpu.SemaphoreType.REGULAR((4,)),
             ],
             compiler_params=pltpu.CompilerParams(
                 collective_id=0, has_side_effects=True, vmem_limit_bytes=32 << 20

time: 50.8 us -> 49.9 us (0.982)
  Pallas kernels: 50 us -> 49.1 us
    pallas_call x1, Pallas kernels: 50 us -> 49.1 us  [on_device(): pl.pallas_call(functools.partial(kernel, n_dp, n_tensor), out_shape=jax.S...]
where the time goes in v6:
time: 49.9 us; the launch traced here: 49.8 us
  Pallas kernels  49.1 us (98%)
  local copies, waits for them, and re-layouts  0.63 us (1%)
    pallas_call x1, Pallas kernels, on_device(): pl.pallas_call(functools.partial(kernel, n_dp, n_tensor), out_shape=jax.S...  49.1 us

profile of v6, /device:TPU:1, one launch (start us, length us, event | category | flops | bytes accessed | tf_op | source)
XLA Modules:
  0.0 49.8 jit_solution(11295318044180535844)
XLA Ops:
  0.0 49.1 %shard_map.64 = bf16[16,2048]{1,0:T(8,128)(2,1)S(1)} custom-call(bf16[256,2048]{1,0:T(8,128)(2,1)} %tok_h.1, bf16[8,176,128]{2,1,0:T(8,128)(2,1)} %bitcast.4, bf16[8,176,128]{2,1,0:T(8,128)(2,1)} %bitcast.5, bf16[8,176,128]{2,1,0:T(8,128)(2,1)} %down_h.1, f32[8,2048]{1,0:T(8,128)} %bitcast.6, f32[16,128]{1,0:T(8,128)} %bitcast.7), custom_call_target="tpu_custom_call" | custom-call | tf_op jit(solution)/shard_map/pallas_call | solution.py:336
  49.2 0.6 %copy.8 = bf16[16,2048]{1,0:T(8,128)(2,1)} copy(bf16[16,2048]{1,0:T(8,128)(2,1)S(1)} %shard_map.64) | data formatting | bytes 131072

commit v7 on v6

--- a/solution.py
+++ b/solution.py
@@ -15,10 +15,11 @@
 STEP = 32
 
 READY = (
-    ((2, 2), (2, 1), (2, 3), (1, 2), (3, 2), (2, 0), (0, 2), (1, 1)),
-    ((3, 3), (1, 3), (3, 1), (1, 0), (3, 0), (0, 1), (0, 3), (0, 0)),
+    ((2, 2), (1, 2), (2, 1), (2, 3), (1, 1), (1, 3), (2, 0), (0, 2)),
+    ((3, 2), (3, 1), (3, 3), (3, 0), (0, 1), (0, 3), (1, 0), (0, 0)),
 )
 OFFSETS = tuple(o for group in READY for o in group if o != (0, 0))
+NEAR = tuple(o for o in OFFSETS if o != (2, 2))
 ALL = OFFSETS + ((0, 0),)
 SLOTS = (((0, 0), (1, 2), (0, 2), (1, 0)), ((0, 1), (1, 3), (0, 3)), ((1, 1),))
 DIRECT = (2,)
@@ -110,9 +111,8 @@
     pl.semaphore_wait(barrier, len(OFFSETS) + 3)
 
     for dx, dy in OFFSETS:
-        copy_to(row_out, row_in.at[d], row_send, row_recv, dp=peer(dx, dy)).start()
+        copy_to(row_out, row_in.at[d], row_send, row_recv.at[int((dx, dy) == (2, 2))], dp=peer(dx, dy)).start()
     wait_all(weights, load_sem.at[3])
-    wait_all(row_in.at[0 : len(OFFSETS)], row_recv)
 
     diag = lax.rem(lax.broadcasted_iota(jnp.int32, (STEP, width), 1), STEP) == lax.broadcasted_iota(
         jnp.int32, (STEP, width), 0
@@ -127,7 +127,8 @@
         )
 
     lefts = []
-    for group in READY:
+    for order, group in enumerate(READY):
+        wait_all(row_in.at[0 : len(NEAR) if order == 0 else 1], row_recv.at[order])
         left = []
         for dx, dy in group:
             src = lax.rem(peer(dx, dy) + n_dp - 1, n_dp)
@@ -356,7 +357,7 @@
                 pltpu.VMEM((2, 2, block, cols), bf16),
                 pltpu.VMEM((n_tensor - 1, block, cols), bf16),
                 dma((4,)),
-                dma(()), dma(()),
+                dma(()), dma((2,)),
                 dma(()), dma((4,)),
                 dma(()), dma((groups,)), dma(()), dma(()),
                 dma(()), dma(()),

time: 49.9 us -> 49.2 us (0.986)
  Pallas kernels: 49.1 us -> 48.5 us
    pallas_call x1, Pallas kernels: 49.1 us -> 48.5 us  [on_device(): pl.pallas_call(functools.partial(kernel, n_dp, n_tensor), out_shape=jax.S...]
where the time goes in v7:
time: 49.2 us; the launch traced here: 49.1 us
  Pallas kernels  48.5 us (99%)
  local copies, waits for them, and re-layouts  0.63 us (1%)
    pallas_call x1, Pallas kernels, on_device(): pl.pallas_call(functools.partial(kernel, n_dp, n_tensor), out_shape=jax.S...  48.5 us

profile of v7, /device:TPU:1, one launch (start us, length us, event | category | flops | bytes accessed | tf_op | source)
XLA Modules:
  0.0 49.1 jit_solution(7827951080656239261)
XLA Ops:
  0.0 48.5 %shard_map.64 = bf16[16,2048]{1,0:T(8,128)(2,1)S(1)} custom-call(bf16[256,2048]{1,0:T(8,128)(2,1)} %tok_h.1, bf16[8,176,128]{2,1,0:T(8,128)(2,1)} %bitcast.4, bf16[8,176,128]{2,1,0:T(8,128)(2,1)} %bitcast.5, bf16[8,176,128]{2,1,0:T(8,128)(2,1)} %down_h.1, f32[8,2048]{1,0:T(8,128)} %bitcast.6, f32[16,128]{1,0:T(8,128)} %bitcast.7), custom_call_target="tpu_custom_call" | custom-call | tf_op jit(solution)/shard_map/pallas_call | solution.py:337
  48.5 0.6 %copy.8 = bf16[16,2048]{1,0:T(8,128)(2,1)} copy(bf16[16,2048]{1,0:T(8,128)(2,1)S(1)} %shard_map.64) | data formatting | bytes 131072

commit v8 on v7

--- a/solution.py
+++ b/solution.py
@@ -77,15 +77,15 @@
         pltpu.make_async_copy(up_h, weights.at[:, ff : 2 * ff, :], load_sem.at[3]),
         pltpu.make_async_copy(down_h, weights.at[:, 2 * ff : 3 * ff, :], load_sem.at[3]),
     ]
-    for load in loads:
-        load.start()
-
     barrier = pltpu.get_barrier_semaphore()
     for dx, dy in OFFSETS:
         pl.semaphore_signal(barrier, inc=1, device_id={"dp": peer(dx, dy)}, device_id_type=MESH)
     neighbours = [z_at(1) * 2 + c, z_at(-1) * 2 + c]
     for tensor in [sibling] + neighbours:
         pl.semaphore_signal(barrier, inc=1, device_id={"tensor": tensor}, device_id_type=MESH)
+
+    for load in loads:
+        load.start()
 
     width = experts * STEP
     spread = lax.broadcasted_iota(jnp.int32, (experts, width), 1) // STEP == lax.broadcasted_iota(
@@ -118,13 +118,15 @@
         jnp.int32, (STEP, width), 0
     )
 
-    def merge(left, first, start):
+    def merge(left, first, starts):
         count = left.shape[0] // STEP
-        right = weights[:, start : start + STEP, :].reshape(width, LANES)
-        both = jnp.dot(left, right, preferred_element_type=jnp.float32)
-        merged[first : first + count, start : start + STEP, :] = both.astype(jnp.bfloat16).reshape(
-            count, STEP, LANES
-        )
+        right = [weights[:, s : s + STEP, :].reshape(width, LANES) for s in starts]
+        both = jnp.dot(left, jnp.concatenate(right, axis=1), preferred_element_type=jnp.float32)
+        both = both.astype(jnp.bfloat16).reshape(count, STEP, -1)
+        for i, s in enumerate(starts):
+            merged[first : first + count, s : s + STEP, :] = both[
+                :, :, i * LANES : (i + 1) * LANES
+            ]
 
     lefts = []
     for order, group in enumerate(READY):
@@ -136,8 +138,8 @@
         left = jnp.concatenate(left, axis=0)
         first = ALL.index(group[0])
         lefts.append((left, first))
-        for start in range(0, 2 * ff, STEP):
-            merge(left, first, start)
+        for start in range(0, 2 * ff, 2 * STEP):
+            merge(left, first, range(start, min(start + 2 * STEP, 2 * ff), STEP))
         for offset in group:
             if offset == (0, 0):
                 continue
@@ -151,8 +153,8 @@
     if starts[-1] + STEP < 3 * ff:
         starts.append(3 * ff - STEP)
     for left, first in lefts:
-        for start in starts:
-            merge(left, first, start)
+        for i in range(0, len(starts), 2):
+            merge(left, first, starts[i : i + 2])
     own_at = len(OFFSETS)
     half_rows = pl.ds(pl.multiple_of(c * ff, 16), ff)
     for g, group in enumerate(SLOTS):

time: 49.2 us -> 49.1 us (level)
  no operation moved by 1% of the time
where the time goes in v8:
time: 49.1 us; the launch traced here: 49 us
  Pallas kernels  48.3 us (98%)
  local copies, waits for them, and re-layouts  0.63 us (1%)
    pallas_call x1, Pallas kernels, on_device(): pl.pallas_call(functools.partial(kernel, n_dp, n_tensor), out_shape=jax.S...  48.3 us

profile of v8, /device:TPU:1, one launch (start us, length us, event | category | flops | bytes accessed | tf_op | source)
XLA Modules:
  0.0 49.0 jit_solution(14294641229094853819)
XLA Ops:
  0.0 48.3 %shard_map.64 = bf16[16,2048]{1,0:T(8,128)(2,1)S(1)} custom-call(bf16[256,2048]{1,0:T(8,128)(2,1)} %tok_h.1, bf16[8,176,128]{2,1,0:T(8,128)(2,1)} %bitcast.4, bf16[8,176,128]{2,1,0:T(8,128)(2,1)} %bitcast.5, bf16[8,176,128]{2,1,0:T(8,128)(2,1)} %down_h.1, f32[8,2048]{1,0:T(8,128)} %bitcast.6, f32[16,128]{1,0:T(8,128)} %bitcast.7), custom_call_target="tpu_custom_call" | custom-call | tf_op jit(solution)/shard_map/pallas_call | solution.py:339
  48.3 0.6 %copy.8 = bf16[16,2048]{1,0:T(8,128)(2,1)} copy(bf16[16,2048]{1,0:T(8,128)(2,1)S(1)} %shard_map.64) | data formatting | bytes 131072
